TPU v7x, 8 devices: a whole 2x2x1 slice. The times are simulated.
8 devices in a mesh: dp: 1 (over z), fsdp: 2 (over y), sp: 4 (over x, core).
Axes of the slice: x: 2, y: 2, z: 1, core: 2. Of those that a mesh axis runs over, the one named last changes fastest.
Arguments:
- x_in: bfloat16 [24, 384, 5120], P(('dp', 'fsdp'), 'sp')
- norm_attn: bfloat16 [5120], P('fsdp')
- w_query: bfloat16 [5120, 5120], P('fsdp')
- w_key: bfloat16 [5120, 5120], P('fsdp')
- w_value: bfloat16 [5120, 5120], P('fsdp')
- w_out: bfloat16 [5120, 5120], P('fsdp')
- norm_mlp: bfloat16 [5120], P('fsdp')
- w_gate: bfloat16 [5120, 13824], P('fsdp')
- w_up: bfloat16 [5120, 13824], P('fsdp')
- w_down: bfloat16 [13824, 5120], P('fsdp')
Outputs:
- output: bfloat16 [24, 384, 5120], P(('dp', 'fsdp'), 'sp')
All inputs are finite; a program needn't handle non-finite values.
Results may differ from a plain program's by a relative error of at most 0.0114603.
Values are sent between devices in bfloat16 or wider.
A program may use at most 1.5 GiB of HBM per device.

v0:
```python
import math
import functools
import jax
import jax.numpy as jnp
from jax import lax
from jax.sharding import PartitionSpec as P

HEAD_DIM = 128
NORM_EPS = 1e-5
ROPE_THETA = 5e7
MASK_VALUE = -1e30


def rms_norm(hidden, gain):
    hid_f32 = hidden.astype(jnp.float32)
    inv_rms = lax.rsqrt(jnp.mean(hid_f32 * hid_f32, axis=-1, keepdims=True) + NORM_EPS)
    return (hid_f32 * inv_rms * gain.astype(jnp.float32)).astype(jnp.bfloat16)


def apply_rope(proj, angles):
    half_dim = proj.shape[-1] // 2
    lower_half = proj[..., :half_dim]
    upper_half = proj[..., half_dim:]
    cos_tab = jnp.cos(angles)[..., None, :]
    sin_tab = jnp.sin(angles)[..., None, :]
    return jnp.concatenate([lower_half * cos_tab - upper_half * sin_tab, upper_half * cos_tab + lower_half * sin_tab], axis=-1)


def rope_angles(token_pos):
    inv_freq = jnp.exp(jnp.arange(HEAD_DIM // 2, dtype=jnp.float32) * (-2.0 * math.log(ROPE_THETA) / HEAD_DIM))
    return token_pos.astype(jnp.float32)[:, None] * inv_freq[None, :]


def gather_weight(weight_shard):
    return lax.all_gather(weight_shard, 'fsdp', axis=0, tiled=True)


def local_layer(x_loc, norm_attn, w_query, w_key, w_value, w_out, norm_mlp, w_gate, w_up, w_down, num_shards):
    num_rows, shard_len, model_dim = x_loc.shape
    head_shape = (num_rows, shard_len, model_dim // HEAD_DIM, HEAD_DIM)
    pos_loc = jnp.arange(shard_len, dtype=jnp.int32) * num_shards + lax.axis_index('sp')
    seq_idx = jnp.arange(num_shards * shard_len, dtype=jnp.int32)
    pos_all = (seq_idx % shard_len) * num_shards + seq_idx // shard_len
    angles = rope_angles(pos_loc)
    normed = rms_norm(x_loc, gather_weight(norm_attn))
    query_rot = apply_rope(jnp.dot(normed, gather_weight(w_query), preferred_element_type=jnp.float32).reshape(head_shape), angles).astype(jnp.bfloat16)
    key_rot = apply_rope(jnp.dot(normed, gather_weight(w_key), preferred_element_type=jnp.float32).reshape(head_shape), angles).astype(jnp.bfloat16)
    value_loc = jnp.dot(normed, gather_weight(w_value), preferred_element_type=jnp.float32).astype(jnp.bfloat16).reshape(head_shape)
    key_all = lax.all_gather(key_rot, 'sp', axis=1, tiled=True)
    value_all = lax.all_gather(value_loc, 'sp', axis=1, tiled=True)
    scores = jnp.einsum('bqhd,bkhd->bhqk', query_rot, key_all, preferred_element_type=jnp.float32) * HEAD_DIM ** -0.5
    allowed = pos_all[None, None, None, :] <= pos_loc[None, None, :, None]
    attn_prob = jax.nn.softmax(jnp.where(allowed, scores, MASK_VALUE), axis=-1).astype(jnp.bfloat16)
    attn_mix = jnp.einsum('bhqk,bkhd->bqhd', attn_prob, value_all, preferred_element_type=jnp.float32).astype(jnp.bfloat16).reshape(num_rows, shard_len, model_dim)
    resid = (x_loc.astype(jnp.float32) + jnp.dot(attn_mix, gather_weight(w_out), preferred_element_type=jnp.float32)).astype(jnp.bfloat16)
    normed_mlp = rms_norm(resid, gather_weight(norm_mlp))
    gate_act = jax.nn.silu(jnp.dot(normed_mlp, gather_weight(w_gate), preferred_element_type=jnp.float32))
    up_proj = jnp.dot(normed_mlp, gather_weight(w_up), preferred_element_type=jnp.float32)
    hidden_mlp = (gate_act * up_proj).astype(jnp.bfloat16)
    return (resid.astype(jnp.float32) + jnp.dot(hidden_mlp, gather_weight(w_down), preferred_element_type=jnp.float32)).astype(jnp.bfloat16)


def solution(mesh):
    row_spec = P(('dp', 'fsdp'), 'sp', None)
    weight_spec = P('fsdp', None)
    gain_spec = P('fsdp')
    in_specs = (row_spec, gain_spec, weight_spec, weight_spec, weight_spec, weight_spec, gain_spec, weight_spec, weight_spec, weight_spec)
    layer_fn = functools.partial(local_layer, num_shards=mesh.shape['sp'])
    return jax.shard_map(layer_fn, mesh=mesh, in_specs=in_specs, out_specs=row_spec, check_vma=False)
```

profile of v0, /device:TPU:0, one launch (start us, length us, event | category | flops | bytes accessed | tf_op | source)
XLA Modules:
  0.0 7970.2 jit_solution(6331237711522873971)
XLA Ops:
  6.5 0.7 all-gather.16.cloned.1.call-update
  7.3 0.7 all-gather.18.cloned.1.call-update
  8.8 5.7 all-gather
  14.6 6.7 fusion.24
  21.3 0.9 multiply_cosine_fusion
  22.2 589.2 %all-gather.16.cloned.1.call-done = bf16[5120,5120]{1,0:T(8,128)(2,1)} async-done(((bf16[2560,5120]{1,0:T(8,128)(2,1)}), bf16[5120,5120]{1,0:T(8,128)(2,1)}) %all-gather.16.cloned.1.call-update) | async-done | bytes 52428816 | tf_op jit(solution)/shard_map/all_gather | solution.py:35
  611.3 72.1 fusion.12
  683.5 20.0 copy.34
  703.5 509.0 %all-gather.18.cloned.1.call-done = bf16[5120,5120]{1,0:T(8,128)(2,1)} async-done(((bf16[2560,5120]{1,0:T(8,128)(2,1)}), bf16[5120,5120]{1,0:T(8,128)(2,1)}) %all-gather.18.cloned.1.call-update) | async-done | bytes 52428816 | tf_op jit(solution)/shard_map/all_gather | solution.py:35
  1212.5 72.3 fusion.10
  1284.9 20.1 copy.35
  1305.0 63.6 fusion.68
  1368.6 55.5 subtract_convert_fusion.1
  1424.1 15.0 pad_maximum_fusion
  1439.2 374.5 %all-gather.12.cloned.1.call-done = bf16[5120,5120]{1,0:T(8,128)(2,1)} async-done(((bf16[2560,5120]{1,0:T(8,128)(2,1)}), bf16[5120,5120]{1,0:T(8,128)(2,1)}) %all-gather.12.cloned.1.call-update) | async-done | bytes 52428816 | tf_op jit(solution)/shard_map/all_gather | solution.py:35
  1813.7 72.3 convert_bitcast_fusion.1
  1886.1 10.5 copy.53
  1897.2 0.7 all-gather.24.cloned.1.call-update
  1899.5 4.4 all-gather.1
  1904.6 187.5 %all-gather.20.cloned.1.call-done = bf16[12,384,40,128]{3,1,2,0:T(8,128)(2,1)} async-done(((bf16[12,96,40,128]{3,1,2,0:T(8,128)(2,1)}), bf16[12,384,40,128]{3,1,2,0:T(8,128)(2,1)}) %all-gather.20.cloned.1.call-update) | async-done | bytes 47185936 | tf_op jit(solution)/shard_map/all_gather | solution.py:49
  2092.1 58.0 fusion.34
  2150.2 68.7 fusion.70
  2218.8 151.7 %all-gather.14.cloned.1.call-done = bf16[12,384,40,128]{3,1,2,0:T(8,128)(2,1)} async-done(((bf16[12,96,40,128]{3,1,2,0:T(8,128)(2,1)}), bf16[12,384,40,128]{3,1,2,0:T(8,128)(2,1)}) %all-gather.14.cloned.1.call-update) | async-done | bytes 47185936 | tf_op jit(solution)/shard_map/all_gather | solution.py:50
  2370.5 41.5 convert_bitcast_fusion
  2412.1 559.5 %all-gather.22.cloned.1.call-done = bf16[5120,5120]{1,0:T(8,128)(2,1)} async-done(((bf16[2560,5120]{1,0:T(8,128)(2,1)}), bf16[5120,5120]{1,0:T(8,128)(2,1)}) %all-gather.22.cloned.1.call-update) | async-done | bytes 52428816 | tf_op jit(solution)/shard_map/all_gather | solution.py:35
  2971.6 72.5 fusion.28
  3044.1 1530.3 %all-gather.24.cloned.1.call-done = bf16[5120,13824]{1,0:T(8,128)(2,1)} async-done(((bf16[2560,13824]{1,0:T(8,128)(2,1)}), bf16[5120,13824]{1,0:T(8,128)(2,1)}) %all-gather.24.cloned.1.call-update) | async-done | bytes 141557776 | tf_op jit(solution)/shard_map/all_gather | solution.py:35
  4574.4 177.9 %fusion.5 = f32[12,96,13824]{2,1,0:T(8,128)} fusion(bf16[5120,13824]{1,0:T(8,128)(2,1)} %all-gather.24.cloned.1.call-done, bf16[12,96,5120]{2,1,0:T(8,128)(2,1)} %get-tuple-element.20, f32[5120]{0:T(1024)S(1)} %bitcast.74, f32[12,96]{1,0:T(8,128)S(1)} %add_rsqrt_fusion), kind=kOutput, calls=%fused_computation.5 | convolution fusion | flops 163098132480 | bytes 217080320 | tf_op jit(solution)/shard_map/dot_general | solution.py:57
  4752.3 1424.9 %all-gather.26.cloned.1.call-done = bf16[5120,13824]{1,0:T(8,128)(2,1)} async-done(((bf16[2560,13824]{1,0:T(8,128)(2,1)}), bf16[5120,13824]{1,0:T(8,128)(2,1)}) %all-gather.26.cloned.1.call-update) | async-done | bytes 141557776 | tf_op jit(solution)/shard_map/all_gather | solution.py:35
  6177.2 185.6 %multiply_convert_fusion.clone.6 = bf16[12,96,13824]{2,1,0:T(8,128)(2,1)} fusion(f32[12,96,13824]{2,1,0:T(8,128)} %fusion.5, bf16[5120,13824]{1,0:T(8,128)(2,1)} %all-gather.26.cloned.1.call-done, bf16[12,96,5120]{2,1,0:T(8,128)(2,1)} %get-tuple-element.20, f32[5120]{0:T(1024)S(1)} %bitcast.75, f32[12,96]{1,0:T(8,128)S(1)} %add_rsqrt_fusion), kind=kOutput, calls=%fused_computation.10.clone.clone.clone.clone.clone.1 | convolution fusion | flops 163193683968 | bytes 248930816 | tf_op jit(solution)/shard_map/dot_general | solution.py:58
  6362.8 1417.2 %all-gather.28.cloned.1.call-done = bf16[13824,5120]{1,0:T(8,128)(2,1)} async-done(((bf16[6912,5120]{1,0:T(8,128)(2,1)}), bf16[13824,5120]{1,0:T(8,128)(2,1)}) %all-gather.28.cloned.1.call-update) | async-done | bytes 141557776 | tf_op jit(solution)/shard_map/all_gather | solution.py:35
  7780.0 183.4 %fusion.31 = bf16[12,96,5120]{2,1,0:T(8,128)(2,1)} fusion(bf16[12,96,5120]{2,1,0:T(8,128)(2,1)} %get-tuple-element.20, bf16[13824,5120]{1,0:T(8,128)(2,1)} %all-gather.28.cloned.1.call-done, bf16[12,96,13824]{2,1,0:T(8,128)(2,1)} %multiply_convert_fusion.clone.6), kind=kOutput, calls=%fused_computation.37 | convolution fusion | flops 163092234240 | bytes 197001216 | tf_op jit(solution)/shard_map/dot_general | solution.py:60
  (36 shorter events, 3.8 us)
Async XLA Ops:
  6.5 604.8 %all-gather.16.cloned.1.call-start = ((), (), s32[]{:S(2)}) async-start(), calls=%async_computation.2 | async-start | bytes 78643200 | tf_op jit(solution)/shard_map/all_gather | solution.py:35
  7.3 1.5 copy-start.3
  7.3 1205.3 %all-gather.18.cloned.1.call-start = ((), (), s32[]{:S(2)}) async-start(), calls=%async_computation.3 | async-start | bytes 78643200 | tf_op jit(solution)/shard_map/all_gather | solution.py:35
  8.0 1805.7 %all-gather.12.cloned.1.call-start = ((), (), s32[]{:S(2)}) async-start(), calls=%async_computation | async-start | bytes 78643200 | tf_op jit(solution)/shard_map/all_gather | solution.py:35
  8.8 2083.4 %all-gather.20.cloned.1.call-start = ((), (), s32[]{:S(2)}) async-start(), calls=%async_computation.4 | async-start | bytes 58982400 | tf_op jit(solution)/shard_map/all_gather | solution.py:49
  1305.0 63.6 copy-start.1
  1305.0 63.6 copy-start.2
  1439.2 931.3 %all-gather.14.cloned.1.call-start = ((), (), s32[]{:S(2)}) async-start(), calls=%async_computation.1 | async-start | bytes 58982400 | tf_op jit(solution)/shard_map/all_gather | solution.py:50
  1896.6 1074.9 %all-gather.22.cloned.1.call-start = ((), (), s32[]{:S(2)}) async-start(), calls=%async_computation.5 | async-start | bytes 78643200 | tf_op jit(solution)/shard_map/all_gather | solution.py:35
  1897.2 2677.2 %all-gather.24.cloned.1.call-start = ((), (), s32[]{:S(2)}) async-start(), calls=%async_computation.6 | async-start | bytes 212336640 | tf_op jit(solution)/shard_map/all_gather | solution.py:35
  1897.9 4279.2 %all-gather.26.cloned.1.call-start = ((), (), s32[]{:S(2)}) async-start(), calls=%async_computation.7 | async-start | bytes 212336640 | tf_op jit(solution)/shard_map/all_gather | solution.py:35
  1898.7 0.8 copy-start.4
  1898.7 5881.3 %all-gather.28.cloned.1.call-start = ((), (), s32[]{:S(2)}) async-start(), calls=%async_computation.8 | async-start | bytes 212336640 | tf_op jit(solution)/shard_map/all_gather | solution.py:35
  2412.1 2162.3 %copy-start = (f32[2,1,2560]{2,1,0:T(1,128)S(1)}, f32[2,1,2560]{2,1,0:T(1,128)}, u32[]{:S(2)}) copy-start(f32[2,1,2560]{2,1,0:T(1,128)} %convert_element_type.65) | copy-start | bytes 61444
Sparse Core Ops, SparseCore 0:
  8.9 602.4 all-gather.15
  612.9 599.6 all-gather.17
  1214.1 599.6 all-gather.11
  1815.1 276.9 all-gather.19
  2093.5 276.9 all-gather.13
  2371.9 599.6 all-gather.21
  2973.1 1601.2 all-gather.23
  4575.9 1601.2 all-gather.25
  6178.7 1601.2 all-gather.27
where the time goes:
time: 7970 us
  waiting for transfers between devices  6750 us (85%)
  matrix products  936 us (12%)
  other arithmetic  148 us (2%)
  local copies, waits for them, and re-layouts  114 us (1%)
    all_gather x7, waiting for transfers between devices, gather_weight(): return lax.all_gather(weight_shard, 'fsdp', axis=0, tiled=True)  6400 us
    all_gather x1, waiting for transfers between devices, local_layer(): key_all = lax.all_gather(key_rot, 'sp', axis=1, tiled=True)  188 us
    dot_general x1, matrix products, local_layer(): jnp.dot(normed_mlp, gather_weight(w_up), preferred_element_type=jnp.float32)  186 us
    dot_general x1, matrix products, local_layer(): jnp.dot(hidden_mlp, gather_weight(w_down), preferred_element_type=jnp.flo...  183 us
    dot_general x1, matrix products, local_layer(): jnp.dot(normed_mlp, gather_weight(w_gate), preferred_element_type=jnp.flo...  178 us
  transfers between devices with their start and end apart: 9, of which 9 were waited for; matrix products, arithmetic and copies ran while one was open for 13% of the time, Pallas kernels for 0%

commit v1 on v0

v1 whole, which is shorter than its diff:
```python
import functools
import math

import jax
import jax.numpy as jnp
from jax import lax
from jax.experimental import pallas as pl
from jax.experimental.pallas import tpu as pltpu
from jax.sharding import PartitionSpec as P

HEAD_DIM = 128
NORM_EPS = 1e-5
ROPE_THETA = 5e7
MASK_VALUE = -1e30

MESH = pl.DeviceIdType.MESH
ANY = pl.BlockSpec(memory_space=pl.ANY)
VM = pl.BlockSpec(memory_space=pltpu.VMEM)
BF16 = jnp.bfloat16
F32 = jnp.float32

SP = 4
NB = 256
GATE_COLS = 512
FULL_CHUNKS = 6
DOWN_COLS = 256
ROW_CHUNKS = 3


def dot(a, b):
    return jnp.dot(a, b, preferred_element_type=F32)


def layer_kernel(
    x, gain, wq, wk, wv, wo, wg, wu, wd, cos, sin, qpos, kpos,
    out, a_all, qkv_rem, wo_rem, gu_rem, wd_rem, qkv, o_own, o_got, hid, b_all, u_own, u_got,
    gain_rem, send_sem, recv_sem, load_sem,
):
    tokens, dim = x.shape
    num_rows, shard_len = o_own.shape[1], o_own.shape[2]
    half, quarter, eighth = dim // 2, dim // 4, dim // 8
    feat = u_own.shape[1]
    half_feat = wd.shape[0]
    tile = tokens // ROW_CHUNKS
    tile_rows = num_rows // ROW_CHUNKS
    last_cols = feat - FULL_CHUNKS * GATE_COLS
    down_chunks = quarter // DOWN_COLS

    y = lax.axis_index("fsdp")
    me = lax.axis_index("sp")
    core, chip = me % 2, me // 2
    peer = [me, me + 1 - 2 * core, (me + 2) % 4, 3 - me]
    to_y = {"fsdp": 1 - y}
    to = [None] + [{"sp": peer[k]} for k in (1, 2, 3)]

    def sp_of(k):
        return 2 * ((chip + k // 2) % 2) + (core + k) % 2

    def cols(start, size):
        return pl.ds(pl.multiple_of(start, 128), size)

    used = [0]

    def slots(n):
        used[0] += n
        return used[0] - n

    s_gain, s_qkv, s_wo, s_gu, s_wd = slots(1), slots(6), slots(4), slots(2 * (FULL_CHUNKS + 1)), slots(4 * down_chunks)
    s_a, s_b = slots(3 * ROW_CHUNKS), slots(3 * ROW_CHUNKS)
    s_o, s_u = slots(3 * ROW_CHUNKS), slots(3 * (FULL_CHUNKS + 1))

    def copy(slot, src, dst, dev):
        return pltpu.make_async_remote_copy(
            src_ref=src, dst_ref=dst, send_sem=send_sem.at[slot], recv_sem=recv_sem.at[slot], device_id=dev, device_id_type=MESH
        )

    def load(slot, src, dst):
        return pltpu.make_async_copy(src, dst, load_sem.at[slot])

    barrier = pltpu.get_barrier_semaphore()
    for dev in (to_y, to[1], to[2], to[3]):
        pl.semaphore_signal(barrier, inc=1, device_id=dev, device_id_type=MESH)
    pl.semaphore_wait(barrier, 4)

    c_gain = copy(s_gain, gain, gain_rem, to_y)
    c_gain.start()

    def qkv_copy(j, h):
        part = (1 - y) if h == 0 else y
        src = (wq, wk, wv)[j].at[:, cols(part * half + me * eighth, eighth)]
        return copy(s_qkv + 2 * j + h, src, qkv_rem.at[j, :, h * eighth : (h + 1) * eighth], to_y)

    def wo_copy(k):
        if k == 0:
            return copy(s_wo, wo.at[:, cols(me * quarter, quarter)], wo_rem.at[0], to_y)
        return copy(s_wo + k, wo_rem.at[k - k % 2 if k == 3 else 0], wo_rem.at[k], to[2] if k == 2 else to[1])

    def gu_copy(c, t, size=GATE_COLS):
        src = (wg, wu)[t].at[:, cols(me * feat + c * GATE_COLS, size)]
        return copy(s_gu + 2 * c + t, src, gu_rem.at[t, :, cols(c * GATE_COLS, size)], to_y)

    def wd_copy(c, k):
        here = cols(c * DOWN_COLS, DOWN_COLS)
        if k == 0:
            return copy(s_wd + 4 * c, wd.at[:, cols(me * quarter + c * DOWN_COLS, DOWN_COLS)], wd_rem.at[0, :, here], to_y)
        src = wd_rem.at[2 if k == 3 else 0, :, here]
        return copy(s_wd + 4 * c + k, src, wd_rem.at[k, :, here], to[2] if k == 2 else to[1])

    for j in range(3):
        for h in range(2):
            qkv_copy(j, h).start()
    wo_copy(0).start()
    for c in range(FULL_CHUNKS + 1):
        for t in range(2):
            gu_copy(c, t, GATE_COLS if c < FULL_CHUNKS else last_cols).start()
    for c in range(down_chunks):
        wd_copy(c, 0).start()
    c_gain.wait_recv()

    def act_copy(base, ref, r, k):
        rows_of = lambda p: pl.ds(p * tokens + r * tile, tile)
        return copy(base + 3 * r + k - 1, ref.at[rows_of(2 if k == 3 else 0)], ref.at[rows_of(k)], to[2] if k == 2 else to[1])

    def norm_chunk(src, dst, which, r):
        rows = tile // 3
        gm = gain[which : which + 1, :]
        go = gain_rem[which : which + 1, :]

        def body(in_ref, out_ref):
            def sub(s, carry):
                here = pl.ds(pl.multiple_of(s * 16, 16), 16)
                mine = in_ref[here, cols(y * half, half)].astype(F32)
                other = in_ref[here, cols((1 - y) * half, half)].astype(F32)
                total = jnp.sum(mine * mine, axis=-1, keepdims=True) + jnp.sum(other * other, axis=-1, keepdims=True)
                inv = lax.rsqrt(total / dim + NORM_EPS)
                out_ref[here, 0:half] = (mine * inv * gm).astype(BF16)
                out_ref[here, half:dim] = (other * inv * go).astype(BF16)
                return carry

            lax.fori_loop(0, rows // 16, sub, 0)

        pltpu.emit_pipeline(
            body,
            grid=(3,),
            in_specs=[pl.BlockSpec((rows, dim), lambda t: (r * 3 + t, 0))],
            out_specs=[pl.BlockSpec((rows, dim), lambda t: (r * 3 + t, 0))],
        )(src, dst)

    def norm_and_send(src, dst, which, base):
        def chunk(r, carry):
            norm_chunk(src, dst, which, r)
            act_copy(base, dst, r, 2).start()
            act_copy(base, dst, r, 1).start()
            return carry

        lax.fori_loop(0, ROW_CHUNKS, chunk, 0)

    def pass_on(base, ref, r):
        act_copy(base, ref, r, 2).wait_recv()
        act_copy(base, ref, r, 3).start()

    def gemm_phases(w_buf):
        def qkv_load(j, slot):
            w = (wq, wk, wv)[j]
            ds = [
                load(4 * slot + h, w.at[:, cols((y if h == 0 else 1 - y) * half + me * eighth, eighth)],
                     w_buf.at[slot, 0:half, h * eighth : (h + 1) * eighth])
                for h in range(2)
            ]
            ds.append(load(4 * slot + 2, qkv_rem.at[j], w_buf.at[slot, half:dim, 0:quarter]))
            return ds

        def qkv_fetch(j, slot):
            ds = qkv_load(j, slot)
            ds[0].start()
            ds[1].start()
            qkv_copy(j, 0).wait_recv()
            qkv_copy(j, 1).wait_recv()
            ds[2].start()
            for d in ds:
                d.wait()

        def qkv_step(s, carry):
            late = s // 4
            j = (1 - late) * (s % 2) + late * 2
            side = (1 - late) * (s // 2) + late * (s % 2)
            slot = j % 2

            @pl.when(s == 0)
            def _():
                pass_on(s_a, a_all, 0)
                qkv_fetch(0, 0)
                for r in range(ROW_CHUNKS):
                    act_copy(s_a, a_all, r, 1).wait_recv()

            @pl.when(s == 1)
            def _():
                pass_on(s_a, a_all, 1)
                pass_on(s_a, a_all, 2)
                qkv_fetch(1, 1)

            @pl.when(s == 2)
            def _():
                for r in range(ROW_CHUNKS):
                    act_copy(s_a, a_all, r, 3).wait_recv()

            @pl.when(s == 4)
            def _():
                qkv_fetch(2, 0)

            def body(a_ref, cos_ref, sin_ref, o_ref):
                c_tab, s_tab = cos_ref[0, 0], sin_ref[0, 0]
                for n in range(quarter // NB):
                    acc = dot(a_ref[...], w_buf[slot, :, n * NB : (n + 1) * NB])
                    for h in range(NB // HEAD_DIM):
                        t = acc[:, h * HEAD_DIM : (h + 1) * HEAD_DIM]
                        rot = t * c_tab + pltpu.roll(t, HEAD_DIM // 2, 1) * s_tab
                        lo = n * NB + h * HEAD_DIM
                        o_ref[0, :, :, lo : lo + HEAD_DIM] = rot.astype(BF16).reshape(tile_rows, shard_len, HEAD_DIM)

            n_t = 2 * ROW_CHUNKS
            t0 = side * n_t
            tab = pl.BlockSpec((1, 1, tile, HEAD_DIM), lambda t: (j // 2, (t0 + t) // ROW_CHUNKS, 0, 0))
            pltpu.emit_pipeline(
                body,
                grid=(n_t,),
                in_specs=[pl.BlockSpec((tile, dim), lambda t: (t0 + t, 0)), tab, tab],
                out_specs=[
                    pl.BlockSpec(
                        (1, tile_rows, shard_len, quarter),
                        lambda t: (j * SP + (t0 + t) // ROW_CHUNKS, (t0 + t) % ROW_CHUNKS, 0, 0),
                    )
                ],
            )(a_all, cos, sin, qkv)
            return carry

        lax.fori_loop(0, 6, qkv_step, 0)

    def attention():
        def o_copy(r, k):
            rows = pl.ds(r * tile_rows, tile_rows)
            return copy(s_o + 3 * r + k - 1, o_own.at[k, rows], o_got.at[k, rows], to[k])

        seq = SP * shard_len

        def body(q_ref, k_ref, v_ref, o_ref):
            keep = kpos[0:1, :] <= qpos[:, 0:1]

            def head(h, carry):
                here = cols(h * HEAD_DIM, HEAD_DIM)
                q = q_ref[:, 0, :, here].reshape(seq, HEAD_DIM)
                k = k_ref[:, 0, :, here].reshape(seq, HEAD_DIM)
                v = v_ref[:, 0, :, here].reshape(seq, HEAD_DIM)
                s = lax.dot_general(q, k, (((1,), (1,)), ((), ())), preferred_element_type=F32) * HEAD_DIM**-0.5
                s = jnp.where(keep, s, MASK_VALUE)
                p = jnp.exp(s - jnp.max(s, axis=-1, keepdims=True))
                total = jnp.sum(p, axis=-1, keepdims=True)
                o = dot(p.astype(BF16), v) / total
                o_ref[:, 0, :, here] = o.astype(BF16).reshape(SP, shard_len, HEAD_DIM)
                return carry

            lax.fori_loop(0, quarter // HEAD_DIM, head, 0)

        def chunk(r, carry):
            def spec(j):
                return pl.BlockSpec((SP, 1, shard_len, quarter), lambda t: (j, r * tile_rows + t, 0, 0))

            pltpu.emit_pipeline(
                body, grid=(tile_rows,), in_specs=[spec(0), spec(1), spec(2)], out_specs=[spec(0)]
            )(qkv, qkv, qkv, o_own)
            for k in (2, 3, 1):
                o_copy(r, k).start()
            return carry

        lax.fori_loop(0, ROW_CHUNKS, chunk, 0)
        return o_copy

    def out_phase(w_buf, o_buf, o_copy):
        def fetch(k, slot):
            return [
                load(4 * slot, wo.at[:, cols(sp_of(k) * quarter, quarter)], w_buf.at[slot, 0:half]),
                load(4 * slot + 1, wo_rem.at[k], w_buf.at[slot, half:dim]),
            ]

        def o_load(k):
            src = o_own if k == 0 else o_got
            return [
                load(8 + 2 * k + h, src.at[k, :, :, h * eighth : (h + 1) * eighth],
                     o_buf.at[:, :, cols(h * half + sp_of(k) * eighth, eighth)])
                for h in range(2)
            ]

        wo_copy(0).wait_recv()
        wo_copy(2).start()
        wo_copy(1).start()
        for d in fetch(0, 0):
            d.start()
        loads = o_load(0)
        for k in (1, 2, 3):
            for r in range(ROW_CHUNKS):
                o_copy(r, k).wait_recv()
            loads += o_load(k)
        for d in loads:
            d.start()
        for d in loads:
            d.wait()

        def step(k, carry):
            slot = k % 2

            @pl.when(k == 1)
            def _():
                wo_copy(2).wait_recv()
                wo_copy(3).start()

            for nxt in range(1, SP):

                @pl.when(k == nxt - 1)
                def _():
                    if nxt != 2:
                        wo_copy(nxt).wait_recv()
                    for d in fetch(nxt, nxt % 2):
                        d.start()

            for d in fetch(k, slot):
                d.wait()

            def body(x_ref, h_ref):
                t = pl.program_id(0)
                lhs = o_buf[pl.ds(t * tile_rows, tile_rows)].reshape(tile, dim)
                for n in range(quarter // NB):
                    here = slice(n * NB, (n + 1) * NB)
                    h_ref[:, here] = (x_ref[:, here].astype(F32) + dot(lhs, w_buf[slot, :, here])).astype(BF16)

            spec = pl.BlockSpec((tile, quarter), lambda t: (t, sp_of(k)))
            pltpu.emit_pipeline(body, grid=(ROW_CHUNKS,), in_specs=[spec], out_specs=[spec])(x, hid)
            return carry

        lax.fori_loop(0, SP, step, 0)

    def gate_phase(w_buf):
        def u_copy(c, k, size=GATE_COLS):
            here = cols(c * GATE_COLS, size)
            return copy(
                s_u + 3 * c + k - 1, u_own.at[pl.ds(k * tokens, tokens), here], u_got.at[pl.ds(k * tokens, tokens), here], to[k]
            )

        def w_load(c, slot, size=GATE_COLS):
            mine = [
                load(4 * slot + t, (wg, wu)[t].at[:, cols(me * feat + c * GATE_COLS, size)],
                     w_buf.at[slot, 0:half, t * size : (t + 1) * size])
                for t in range(2)
            ]
            other = [
                load(4 * slot + 2 + t, gu_rem.at[t, :, cols(c * GATE_COLS, size)],
                     w_buf.at[slot, half:dim, t * size : (t + 1) * size])
                for t in range(2)
            ]
            return mine, other

        def run(c, side, slot, size):
            def body(b_ref, o_ref):
                parts = [dot(b_ref[...], w_buf[slot, :, n * NB : (n + 1) * NB]) for n in range(2 * size // NB)]
                if size % NB:
                    g = [parts[0], parts[1][:, :128]]
                    u = [jnp.concatenate([parts[1][:, 128:], parts[2][:, :128]], axis=1), parts[2][:, 128:]]
                else:
                    g, u = parts[: size // NB], parts[size // NB :]
                lo = 0
                for gg, uu in zip(g, u):
                    o_ref[:, lo : lo + gg.shape[1]] = (jax.nn.silu(gg) * uu).astype(BF16)
                    lo += gg.shape[1]

            n_t = 2 * ROW_CHUNKS
            pltpu.emit_pipeline(
                body,
                grid=(n_t,),
                in_specs=[pl.BlockSpec((tile, dim), lambda t: (side * n_t + t, 0))],
                out_specs=[pl.BlockSpec((tile, size), lambda t: (side * n_t + t, 0))],
            )(b_all, u_own.at[:, cols(c * GATE_COLS, size)])

            @pl.when(side == 0)
            def _():
                u_copy(c, 1, size).start()

            @pl.when(side == 1)
            def _():
                u_copy(c, 2, size).start()
                u_copy(c, 3, size).start()

        early = FULL_CHUNKS // 2

        def which(s):
            q = s // FULL_CHUNKS
            c = (1 - q) * (s % early) + q * (early + (s - FULL_CHUNKS) // 2)
            side = (1 - q) * (s // early) + q * (s % 2)
            return c, side

        first_mine, _ = w_load(0, 0)
        for d in first_mine:
            d.start()
        total = 2 * FULL_CHUNKS

        def step(s, carry):
            c, side = which(s)
            slot = s % 2
            mine, other = w_load(c, slot)

            for r in range(ROW_CHUNKS):

                @pl.when(s == r + 1)
                def _():
                    pass_on(s_b, b_all, r)

            @pl.when(side == 0)
            def _():
                gu_copy(c, 0).wait_recv()
                gu_copy(c, 1).wait_recv()

            for d in other:
                d.start()

            @pl.when(s == 0)
            def _():
                for r in range(ROW_CHUNKS):
                    act_copy(s_b, b_all, r, 1).wait_recv()

            @pl.when(s == early)
            def _():
                for r in range(ROW_CHUNKS):
                    act_copy(s_b, b_all, r, 3).wait_recv()

            for d in mine + other:
                d.wait()

            @pl.when(s + 1 < total)
            def _():
                nc, _ = which(s + 1)
                for d in w_load(nc, (s + 1) % 2)[0]:
                    d.start()

            run(c, side, slot, GATE_COLS)
            return carry

        lax.fori_loop(0, total, step, 0)

        mine, other = w_load(FULL_CHUNKS, 0, last_cols)
        for d in mine:
            d.start()
        for t in range(2):
            gu_copy(FULL_CHUNKS, t, last_cols).wait_recv()
        for d in other:
            d.start()
        for d in mine + other:
            d.wait()

        def last(side, carry):
            run(FULL_CHUNKS, side, 0, last_cols)
            return carry

        lax.fori_loop(0, 2, last, 0)
        return u_copy

    def down_phase(u_copy, u_buf, w_mine, w_other, h_buf, o_buf):
        def u_load(k):
            sp = sp_of(k)
            at = ((sp // 2 + y) % 2) * half_feat + (sp % 2) * feat
            src = u_own if k == 0 else u_got
            return load(k, src.at[pl.ds(k * tokens, tokens)], u_buf.at[:, cols(at, feat)])

        u_load(0).start()
        for k in (1, 2, 3):
            for c in range(FULL_CHUNKS + 1):
                u_copy(c, k, GATE_COLS if c < FULL_CHUNKS else last_cols).wait_recv()
            u_load(k).start()

        def out_cols(c, k):
            return cols(sp_of(k) * quarter + c * DOWN_COLS, DOWN_COLS)

        def fetch(c, k, slot):
            here = out_cols(c, k)
            return [load(4 + 2 * slot, wd.at[:, here], w_mine.at[slot]), load(5 + 2 * slot, hid.at[:, here], h_buf.at[slot])]

        def store(c, k, slot):
            return load(8 + slot, o_buf.at[slot], out.at[:, out_cols(c, k)])

        for d in fetch(0, 0, 0):
            d.start()
        for k in range(SP):
            u_load(k).wait()
        total = SP * down_chunks

        def step(n, carry):
            c, k = unit_of(n)
            slot = n % 2

            @pl.when(k == 0)
            def _():
                wd_copy(c, 0).wait_recv()
                wd_copy(c, 2).start()
                wd_copy(c, 1).start()

            @pl.when(k == 1)
            def _():
                wd_copy(c, 1).wait_recv()

            @pl.when(k == 2)
            def _():
                wd_copy(c, 2).wait_recv()
                wd_copy(c, 3).start()

            @pl.when(k == 3)
            def _():
                wd_copy(c, 3).wait_recv()

            rem = load(10, wd_rem.at[k, :, cols(c * DOWN_COLS, DOWN_COLS)], w_other)
            rem.start()

            @pl.when(n + 1 < total)
            def _():
                nc, nk = unit_of(n + 1)
                for d in fetch(nc, nk, (n + 1) % 2):
                    d.start()

            for d in fetch(c, k, slot):
                d.wait()
            acc = h_buf[slot].astype(F32) + dot(u_buf[:, 0:half_feat], w_mine[slot])
            rem.wait()
            acc = acc + dot(u_buf[:, half_feat:], w_other[...])

            @pl.when(n >= 2)
            def _():
                pc, pk = unit_of(n - 2)
                store(pc, pk, slot).wait()

            o_buf[slot] = acc.astype(BF16)
            store(c, k, slot).start()
            return carry

        def unit_of(n):
            tail = (n + 2) // total
            head = (total + 1 - n) // total
            m = n - 2
            b, u = m // 4, m % 4
            c = head * 0 + tail * (down_chunks - 1) + (1 - head) * (1 - tail) * (b + 1 - u // 2)
            k = head * n + tail * (2 + n - (total - 2)) + (1 - head) * (1 - tail) * u
            return c, k

        lax.fori_loop(0, total, step, 0)
        for n in (total - 2, total - 1):
            store(down_chunks - 1, 2 + n - (total - 2), n % 2).wait()

    norm_and_send(x, a_all, 0, s_a)
    pl.run_scoped(gemm_phases, pltpu.VMEM((2, dim, quarter), BF16))
    o_copy = attention()
    pl.run_scoped(
        functools.partial(out_phase, o_copy=o_copy),
        pltpu.VMEM((2, dim, quarter), BF16),
        pltpu.VMEM((num_rows, shard_len, dim), BF16),
    )
    norm_and_send(hid, b_all, 1, s_b)
    saved = []

    def gates(w_buf):
        saved.append(gate_phase(w_buf))

    pl.run_scoped(gates, pltpu.VMEM((2, dim, 2 * GATE_COLS), BF16))
    pl.run_scoped(
        functools.partial(down_phase, saved[0]),
        pltpu.VMEM((tokens, 2 * half_feat), BF16),
        pltpu.VMEM((2, half_feat, DOWN_COLS), BF16),
        pltpu.VMEM((half_feat, DOWN_COLS), BF16),
        pltpu.VMEM((2, tokens, DOWN_COLS), BF16),
        pltpu.VMEM((2, tokens, DOWN_COLS), BF16),
    )

    c_gain.wait_send()
    for j in range(3):
        for h in range(2):
            qkv_copy(j, h).wait_send()
    for k in range(SP):
        wo_copy(k).wait_send()
    u_copy = saved[0]
    for c in range(FULL_CHUNKS + 1):
        size = GATE_COLS if c < FULL_CHUNKS else last_cols
        for t in range(2):
            gu_copy(c, t, size).wait_send()
        for k in (1, 2, 3):
            u_copy(c, k, size).wait_send()
    for c in range(down_chunks):
        for k in range(SP):
            wd_copy(c, k).wait_send()
    for r in range(ROW_CHUNKS):
        for k in (1, 2, 3):
            act_copy(s_a, a_all, r, k).wait_send()
            act_copy(s_b, b_all, r, k).wait_send()
            o_copy(r, k).wait_send()


def tables(shard_len, tile_rows):
    me = lax.axis_index("sp")
    peer = jnp.stack([me, me ^ 1, me ^ 2, me ^ 3])
    pos = jnp.arange(shard_len, dtype=jnp.int32)[None, :] * SP + peer[:, None]
    inv_freq = jnp.exp(jnp.arange(HEAD_DIM // 2, dtype=F32) * (-2.0 * math.log(ROPE_THETA) / HEAD_DIM))
    angles = pos.astype(F32)[..., None] * inv_freq
    cos_tab, sin_tab = jnp.cos(angles), jnp.sin(angles)
    cos = jnp.tile(jnp.concatenate([cos_tab, cos_tab], axis=-1), (1, tile_rows, 1))
    sin = jnp.tile(jnp.concatenate([-sin_tab, sin_tab], axis=-1), (1, tile_rows, 1))
    cos = jnp.stack([cos, jnp.ones_like(cos)])
    sin = jnp.stack([sin, jnp.zeros_like(sin)])
    flat = pos.reshape(-1)
    qpos = jnp.broadcast_to(flat[:, None], (flat.size, 128))
    kpos = jnp.broadcast_to(flat[None, :], (8, flat.size))
    return cos, sin, qpos, kpos


def local_layer(x_loc, norm_attn, w_query, w_key, w_value, w_out, norm_mlp, w_gate, w_up, w_down):
    num_rows, shard_len, dim = x_loc.shape
    tokens = num_rows * shard_len
    half, quarter = dim // 2, dim // 4
    half_feat = w_down.shape[0]
    feat = half_feat // 2
    gain = jnp.zeros((8, half), F32).at[0].set(norm_attn.astype(F32)).at[1].set(norm_mlp.astype(F32))
    cos, sin, qpos, kpos = tables(shard_len, num_rows // ROW_CHUNKS)

    def buf(*shape):
        return jax.ShapeDtypeStruct(shape, BF16)

    shapes = [
        buf(tokens, dim),
        buf(SP * tokens, dim),
        buf(3, half, quarter),
        buf(SP, half, quarter),
        buf(2, half, feat),
        buf(SP, half_feat, quarter),
        buf(3 * SP, num_rows, shard_len, quarter),
        buf(SP, num_rows, shard_len, quarter),
        buf(SP, num_rows, shard_len, quarter),
        buf(tokens, dim),
        buf(SP * tokens, dim),
        buf(SP * tokens, feat),
        buf(SP * tokens, feat),
    ]
    copies = 1 + 6 + 4 + 2 * (FULL_CHUNKS + 1) + 4 * (quarter // DOWN_COLS) + 9 * ROW_CHUNKS + 3 * (FULL_CHUNKS + 1)
    outs = pl.pallas_call(
        layer_kernel,
        out_shape=shapes,
        in_specs=[ANY, VM] + [ANY] * 9 + [VM, VM],
        out_specs=[ANY] * len(shapes),
        scratch_shapes=[
            pltpu.VMEM((8, half), F32),
            pltpu.SemaphoreType.DMA((copies,)),
            pltpu.SemaphoreType.DMA((copies,)),
            pltpu.SemaphoreType.DMA((16,)),
        ],
        compiler_params=pltpu.CompilerParams(collective_id=0, has_side_effects=True, vmem_limit_bytes=67043328),
        name="decoder_layer",
    )(x_loc.reshape(tokens, dim), gain, w_query, w_key, w_value, w_out, w_gate, w_up, w_down, cos, sin, qpos, kpos)
    return outs[0].reshape(x_loc.shape)


def solution(mesh):
    row_spec = P(("dp", "fsdp"), "sp", None)
    weight_spec = P("fsdp", None)
    gain_spec = P("fsdp")
    in_specs = (row_spec, gain_spec, weight_spec, weight_spec, weight_spec, weight_spec, gain_spec, weight_spec, weight_spec, weight_spec)
    fn = jax.shard_map(local_layer, mesh=mesh, in_specs=in_specs, out_specs=row_spec, check_vma=False)

    def run(*args):
        with jax.sharding.use_abstract_mesh(mesh.abstract_mesh):
            return fn(*args)

    return run
```

time: 7970 us -> 1940 us (0.24)
  waiting for transfers between devices: 6750 us -> 0 us
  Pallas kernels: 0 us -> 1920 us
  matrix products: 936 us -> 0 us
  other arithmetic: 148 us -> 1.11 us
  local copies, waits for them, and re-layouts: 114 us -> 15.8 us
    all_gather x9 -> x0, waiting for transfers between devices: 6740 us -> none  [the longest x7 6400 us: gather_weight(): return lax.all_gather(weight_shard, 'fsdp', axis=0, tiled=True)]
    pallas_call x0 -> x1, Pallas kernels: none -> 1920 us  [local_layer(): pl.pallas_call(layer_kernel, out_shape=shapes, in_specs=[ANY, VM] + [ANY]...]
    dot_general x9 -> x0, matrix products: 936 us -> none  [the longest x1 186 us: local_layer(): jnp.dot(normed_mlp, gather_weight(w_up), preferred_element_type=jnp.float32)]
  transfers between devices with their start and end apart: 9 -> 0, of which waited for: 9 -> 0; matrix products, arithmetic and copies ran while one was open for 13% -> 0% of each run, Pallas kernels for 0% -> 0%
where the time goes in v1:
time: 1940 us
  Pallas kernels  1920 us (99%)
    pallas_call x1, Pallas kernels, local_layer(): pl.pallas_call(layer_kernel, out_shape=shapes, in_specs=[ANY, VM] + [ANY]...  1920 us

profile of v1, /device:TPU:0, one launch (start us, length us, event | category | flops | bytes accessed | tf_op | source)
XLA Modules:
  0.0 1938.7 jit_solution(748938282325916443)
XLA Ops:
  0.0 0.1 pad_add_fusion
  0.1 0.1 broadcast_add_fusion
  0.2 0.1 add.41
  0.2 0.7 reshape.139
  1.0 0.7 reshape.142
  1.7 0.6 broadcast_in_dim.5.kpos
  2.3 0.2 scatter.14.gain
  2.5 0.0 copy-start
  2.5 0.8 broadcast_in_dim.4.qpos
  3.3 0.8 fusion
  4.1 0.2 pad_maximum_fusion
  4.3 0.1 tile.16
  4.3 1.2 stack.26.cos
  5.6 0.1 tile.18
  5.7 0.0 copy-done
  5.7 1.3 stack.27.sin
  7.0 1921.7 %decoder_layer.1 = (bf16[1152,5120]{1,0:T(8,128)(2,1)}, bf16[4608,5120]{1,0:T(8,128)(2,1)}, bf16[3,2560,1280]{2,1,0:T(8,128)(2,1)}, bf16[4,2560,1280]{2,1,0:T(8,...) custom-call(bf16[1152,5120]{1,0:T(8,128)(2,1)} %bitcast.8, ...), custom_call_target="tpu_custom_call" | custom-call | tf_op jit(solution)/shard_map/decoder_layer/pallas_call | solution.py:645
  1928.7 10.0 copy.13
  (3 shorter events, 0.0 us)
Async XLA Ops:
  2.5 3.1 copy-start

commit v2 on v0

v2 whole, which is shorter than its diff:
```python
import functools
import math

import jax
import jax.numpy as jnp
import numpy as np
from jax import lax
from jax.experimental import pallas as pl
from jax.experimental.pallas import tpu as pltpu
from jax.sharding import PartitionSpec as P

HEAD_DIM = 128
NORM_EPS = 1e-5
ROPE_THETA = 5e7
MASK_VALUE = -1e30

MESH = pl.DeviceIdType.MESH
ANY = pl.BlockSpec(memory_space=pl.ANY)
VM = pl.BlockSpec(memory_space=pltpu.VMEM)
BF16 = jnp.bfloat16
F32 = jnp.float32

SP = 4
NB = 256
GATE_COLS = 384
FULL_CHUNKS = 8
DOWN_COLS = 256
DOWN_PARTS = 4
ROW_CHUNKS = 3


def dot(a, b):
    return jnp.dot(a, b, preferred_element_type=F32)


def layer_kernel(
    x, gain, wq, wk, wv, wo, wg, wu, wd, cos, sin,
    out, x_got, a_all, qkv_rem, wo_rem, gu_rem, wd_rem, qkv, o_own, o_got, hid, b_all, u_own, u_got,
    gain_rem, cos_buf, sin_buf, send_sem, recv_sem, load_sem,
):
    tokens, dim = x.shape
    num_rows, shard_len = o_own.shape[1], o_own.shape[2]
    half, quarter, eighth = dim // 2, dim // 4, dim // 8
    feat = u_own.shape[1]
    half_feat = wd.shape[0]
    tile = tokens // ROW_CHUNKS
    tile_rows = num_rows // ROW_CHUNKS
    down_chunks = quarter // DOWN_COLS
    part_rows = half_feat // DOWN_PARTS
    heads = eighth // HEAD_DIM
    rest = feat - FULL_CHUNKS * GATE_COLS
    sizes = [GATE_COLS] * FULL_CHUNKS + [rest - 128, 128]
    starts = [GATE_COLS * c for c in range(FULL_CHUNKS)] + [feat - rest, feat - 128]
    chunks = len(sizes)

    y = lax.axis_index("fsdp")
    me = lax.axis_index("sp")
    core, chip = me % 2, me // 2
    peer = [me, me + 1 - 2 * core, (me + 2) % 4, 3 - me]
    to_y = {"fsdp": 1 - y}
    to = [None] + [{"sp": peer[k]} for k in (1, 2, 3)]

    def sp_of(k):
        return 2 * ((chip + k // 2) % 2) + (core + k) % 2

    def cols(start, size):
        return pl.ds(pl.multiple_of(start, 128), size)

    def rows(start, size):
        return pl.ds(pl.multiple_of(start, 16), size)

    used = [0]

    def slots(n):
        used[0] += n
        return used[0] - n

    s_gain, s_qkv, s_wo, s_gu = slots(1), slots(6), slots(4), slots(2 * chunks)
    s_wd = slots(4 * DOWN_PARTS * down_chunks)
    s_x, s_a, s_b = slots(ROW_CHUNKS), slots(2 * ROW_CHUNKS), slots(2 * ROW_CHUNKS)
    s_o, s_u = slots(12 * ROW_CHUNKS), slots(3 * chunks)

    def copy(slot, src, dst, dev):
        return pltpu.make_async_remote_copy(
            src_ref=src, dst_ref=dst, send_sem=send_sem.at[slot], recv_sem=recv_sem.at[slot], device_id=dev, device_id_type=MESH
        )

    def load(slot, src, dst):
        return pltpu.make_async_copy(src, dst, load_sem.at[slot])

    barrier = pltpu.get_barrier_semaphore()
    for dev in (to_y, to[1], to[2], to[3]):
        pl.semaphore_signal(barrier, inc=1, device_id=dev, device_id_type=MESH)
    pl.semaphore_wait(barrier, 4)

    def x_copy(r):
        here = rows(r * tile, tile)
        return copy(s_x + r, x.at[here], x_got.at[here], to[2])

    gain_copy = copy(s_gain, gain, gain_rem, to_y)

    def qkv_copy(j, h):
        part = (1 - y + h) % 2
        src = (wq, wk, wv)[j].at[:, cols(part * half + me * eighth, eighth)]
        return copy(s_qkv + 2 * j + h, src, qkv_rem.at[2 * j + h], to_y)

    def wo_copy(k):
        if k == 0:
            return copy(s_wo, wo.at[:, cols(me * quarter, quarter)], wo_rem.at[0], to_y)
        return copy(s_wo + k, wo_rem.at[2 if k == 3 else 0], wo_rem.at[k], to[2] if k == 2 else to[1])

    def gu_copy(c, t, start, size):
        src = (wg, wu)[t].at[:, cols(me * feat + start, size)]
        return copy(s_gu + 2 * c + t, src, gu_rem.at[t, :, cols(start, size)], to_y)

    def wd_copy(m, k):
        part, col = rows((m % DOWN_PARTS) * part_rows, part_rows), (m // DOWN_PARTS) * DOWN_COLS
        if k == 0:
            return copy(s_wd + 4 * m, wd.at[part, cols(me * quarter + col, DOWN_COLS)], wd_rem.at[0, part, cols(col, DOWN_COLS)], to_y)
        here = (part, cols(col, DOWN_COLS))
        return copy(s_wd + 4 * m + k, wd_rem.at[(2 if k == 3 else 0, *here)], wd_rem.at[(k, *here)], to[2] if k == 2 else to[1])

    def act_copy(base, ref, piece, r):
        return copy(
            base + (piece // 2) * ROW_CHUNKS + r,
            ref.at[rows(piece * tokens + r * tile, tile)],
            ref.at[rows((piece + 1) * tokens + r * tile, tile)],
            to[1],
        )

    def o_copy(h, r, k, s):
        here = pl.ds(r * tile_rows, tile_rows)
        piece = k ^ (2 * s)
        return copy(
            s_o + ((h * ROW_CHUNKS + r) * 3 + k - 1) * 2 + s,
            o_own.at[4 * h + piece, here],
            o_got.at[6 * h + 2 * (k - 1) + s, here],
            to[k],
        )

    def u_copy(c, k, start, size):
        here = (pl.ds(k * tokens, tokens), cols(start, size))
        return copy(s_u + 3 * c + k - 1, u_own.at[here], u_got.at[here], to[k])

    for r in range(ROW_CHUNKS):
        x_copy(r).start()
    gain_copy.start()
    for h in range(2):
        for j in range(3):
            qkv_copy(j, h).start()
    wo_copy(0).start()
    for c in range(chunks):
        for t in range(2):
            gu_copy(c, t, starts[c], sizes[c]).start()
    for m in range(DOWN_PARTS * down_chunks):
        wd_copy(m, 0).start()
    tabs = [load(0, cos, cos_buf), load(1, sin, sin_buf)]
    for d in tabs:
        d.start()
    for d in tabs:
        d.wait()
    gain_copy.wait_recv()

    def norm_chunk(src, dst, which, src_row, dst_row):
        n = tile // 3
        gm = gain[which : which + 1, :]
        go = gain_rem[which : which + 1, :]

        def body(in_ref, out_ref):
            def sub(s, carry):
                here = pl.ds(pl.multiple_of(s * 16, 16), 16)
                mine = in_ref[here, cols(y * half, half)].astype(F32)
                other = in_ref[here, cols((1 - y) * half, half)].astype(F32)
                total = jnp.sum(mine * mine, axis=-1, keepdims=True) + jnp.sum(other * other, axis=-1, keepdims=True)
                inv = lax.rsqrt(total / dim + NORM_EPS)
                out_ref[here, 0:half] = (mine * inv * gm).astype(BF16)
                out_ref[here, half:dim] = (other * inv * go).astype(BF16)
                return carry

            lax.fori_loop(0, n // 16, sub, 0)

        pltpu.emit_pipeline(
            body,
            grid=(3,),
            in_specs=[pl.BlockSpec((n, dim), lambda t: (src_row // n + t, 0))],
            out_specs=[pl.BlockSpec((n, dim), lambda t: (dst_row // n + t, 0))],
        )(src, dst)

    def own_a(r, carry):
        norm_chunk(x, a_all, 0, r * tile, r * tile)
        act_copy(s_a, a_all, 0, r).start()
        return carry

    def got_a(r, carry):
        x_copy(r).wait_recv()
        norm_chunk(x_got, a_all, 0, r * tile, 2 * tokens + r * tile)
        act_copy(s_a, a_all, 2, r).start()
        return carry

    def attention(w_qk, w_v):
        seq = SP * shard_len
        idx = lax.broadcasted_iota(jnp.int32, (1, seq), 1)
        idq = lax.broadcasted_iota(jnp.int32, (seq, 1), 0)

        def position(i):
            piece = (i >= shard_len).astype(jnp.int32) + (i >= 2 * shard_len).astype(jnp.int32) + (i >= 3 * shard_len).astype(jnp.int32)
            chip_of = (chip + (piece >> 1)) & 1
            core_of = (core + piece) & 1
            return SP * (i - shard_len * piece) + 2 * chip_of + core_of

        def attn_body(q_ref, k_ref, v_ref, o_ref):
            keep = position(idx) <= position(idq)

            def head(h, carry):
                here = cols(h * HEAD_DIM, HEAD_DIM)
                q = q_ref[:, 0, :, here].reshape(seq, HEAD_DIM)
                k = k_ref[:, 0, :, here].reshape(seq, HEAD_DIM)
                v = v_ref[:, 0, :, here].reshape(seq, HEAD_DIM)
                s = lax.dot_general(q, k, (((1,), (1,)), ((), ())), preferred_element_type=F32) * HEAD_DIM**-0.5
                s = jnp.where(keep, s, MASK_VALUE)
                p = jnp.exp(s - jnp.max(s, axis=-1, keepdims=True))
                total = jnp.sum(p, axis=-1, keepdims=True)
                o = dot(p.astype(BF16), v) / total
                o_ref[:, 0, :, here] = o.astype(BF16).reshape(SP, shard_len, HEAD_DIM)
                return carry

            lax.fori_loop(0, heads, head, 0)

        def w_loads(j, h, dst, at):
            part = (y + h) % 2
            return [
                load(2 * j, (wq, wk, wv)[j].at[:, cols(part * half + me * eighth, eighth)], dst.at[0:half, at : at + eighth]),
                load(2 * j + 1, qkv_rem.at[2 * j + h], dst.at[half:dim, at : at + eighth]),
            ]

        def heads_half(h, carry):
            @pl.when(h == 0)
            def _():
                got_a(0, 0)

            loads = w_loads(0, h, w_qk, 0) + w_loads(1, h, w_qk, eighth)
            loads[0].start()
            loads[2].start()
            qkv_copy(0, h).wait_recv()
            loads[1].start()
            qkv_copy(1, h).wait_recv()
            loads[3].start()
            for d in loads:
                d.wait()

            def qk_side(side, c2):
                @pl.when((h == 0) & (side == 0))
                def _():
                    for r in range(ROW_CHUNKS):
                        act_copy(s_a, a_all, 0, r).wait_recv()

                @pl.when((h == 0) & (side == 1))
                def _():
                    lax.fori_loop(1, ROW_CHUNKS, got_a, 0)
                    for r in range(ROW_CHUNKS):
                        act_copy(s_a, a_all, 2, r).wait_recv()

                t0 = side * 2 * ROW_CHUNKS

                def body(a_ref, q_ref, k_ref):
                    sp = sp_of((t0 + pl.program_id(0)) // ROW_CHUNKS)
                    c_tab, s_tab = cos_buf[sp], sin_buf[sp]
                    for n in range(2 * eighth // NB):
                        acc = dot(a_ref[...], w_qk[:, n * NB : (n + 1) * NB])
                        for i in range(NB // HEAD_DIM):
                            t = acc[:, i * HEAD_DIM : (i + 1) * HEAD_DIM]
                            turned = pltpu.roll(t, HEAD_DIM // 2, 1)
                            shape = (tile_rows, shard_len, HEAD_DIM)
                            rot = t.reshape(shape) * c_tab + turned.reshape(shape) * s_tab
                            lo = n * NB + i * HEAD_DIM
                            ref = q_ref if lo < eighth else k_ref
                            lo = lo % eighth
                            ref[0, :, :, lo : lo + HEAD_DIM] = rot.astype(BF16)

                def spec(j):
                    return pl.BlockSpec(
                        (1, tile_rows, shard_len, eighth),
                        lambda t: ((2 * j + h) * SP + (t0 + t) // ROW_CHUNKS, (t0 + t) % ROW_CHUNKS, 0, 0),
                    )

                pltpu.emit_pipeline(
                    body,
                    grid=(2 * ROW_CHUNKS,),
                    in_specs=[pl.BlockSpec((tile, dim), lambda t: (t0 + t, 0))],
                    out_specs=[spec(0), spec(1)],
                )(a_all, qkv, qkv)
                return c2

            v_loads = w_loads(2, h, w_v, 0)
            v_loads[0].start()
            lax.fori_loop(0, 2, qk_side, 0)
            qkv_copy(2, h).wait_recv()
            v_loads[1].start()
            for d in v_loads:
                d.wait()

            def rows_chunk(r, c2):
                def v_body(a_ref, v_ref):
                    for lo in range(0, eighth, NB):
                        size = min(NB, eighth - lo)
                        acc = dot(a_ref[...], w_v[:, lo : lo + size])
                        v_ref[0, :, :, lo : lo + size] = acc.astype(BF16).reshape(tile_rows, shard_len, size)

                pltpu.emit_pipeline(
                    v_body,
                    grid=(SP,),
                    in_specs=[pl.BlockSpec((tile, dim), lambda t: (t * ROW_CHUNKS + r, 0))],
                    out_specs=[pl.BlockSpec((1, tile_rows, shard_len, eighth), lambda t: ((4 + h) * SP + t, r, 0, 0))],
                )(a_all, qkv)

                def spec(block):
                    return pl.BlockSpec((SP, 1, shard_len, eighth), lambda t: (block, r * tile_rows + t, 0, 0))

                pltpu.emit_pipeline(
                    attn_body,
                    grid=(tile_rows,),
                    in_specs=[spec(h), spec(2 + h), spec(4 + h)],
                    out_specs=[spec(h)],
                )(qkv, qkv, qkv, o_own)
                for k in (2, 3, 1):
                    for s in range(2):
                        o_copy(h, r, k, s).start()
                return c2

            lax.fori_loop(0, ROW_CHUNKS, rows_chunk, 0)
            return carry

        lax.fori_loop(0, 2, heads_half, 0)

    def out_phase(w_buf, o_buf):
        def fetch(k, slot):
            return [
                load(2 * slot, wo.at[:, cols(sp_of(k) * quarter, quarter)], w_buf.at[slot, 0:half]),
                load(2 * slot + 1, wo_rem.at[k], w_buf.at[slot, half:dim]),
            ]

        def o_load(h, k, s):
            src = o_own.at[4 * h + 2 * s] if k == 0 else o_got.at[6 * h + 2 * (k - 1) + s]
            dst = o_buf.at[s * num_rows : (s + 1) * num_rows, :, cols(h * half + sp_of(k) * eighth, eighth)]
            return load(4 + 8 * h + 2 * k + s, src, dst)

        loads = []

        def o_fetch(h):
            for k in (0, 1, 2, 3):
                for s in range(2):
                    if k:
                        for r in range(ROW_CHUNKS):
                            o_copy(h, r, k, s).wait_recv()
                    d = o_load(h, k, s)
                    d.start()
                    loads.append(d)

        o_fetch(0)
        wo_copy(0).wait_recv()
        wo_copy(2).start()
        wo_copy(1).start()
        for d in fetch(0, 0):
            d.start()
        o_fetch(1)
        for d in loads:
            d.wait()

        def step(k, carry):
            slot = k % 2

            @pl.when(k == 0)
            def _():
                wo_copy(1).wait_recv()
                for d in fetch(1, 1):
                    d.start()

            @pl.when(k == 2)
            def _():
                wo_copy(2).wait_recv()
                wo_copy(3).start()
                for d in fetch(2, 0):
                    d.start()

            for d in fetch(k, slot):
                d.wait()

            def run(x_ref_all, s):
                def body(x_ref, h_ref):
                    mine = pl.ds(s * num_rows + pl.program_id(0) * tile_rows, tile_rows)
                    for n in range(quarter // NB):
                        here = slice(n * NB, (n + 1) * NB)
                        lhs = o_buf[mine].reshape(tile, dim)
                        h_ref[:, here] = (x_ref[:, here].astype(F32) + dot(lhs, w_buf[slot, :, here])).astype(BF16)

                pltpu.emit_pipeline(
                    body,
                    grid=(ROW_CHUNKS,),
                    in_specs=[pl.BlockSpec((tile, quarter), lambda t: (t, sp_of(k)))],
                    out_specs=[pl.BlockSpec((tile, quarter), lambda t: (s * ROW_CHUNKS + t, sp_of(k)))],
                )(x_ref_all, hid)

            run(x, 0)

            @pl.when(k == 2)
            def _():
                wo_copy(3).wait_recv()
                for d in fetch(3, 1):
                    d.start()

            run(x_got, 1)
            return carry

        lax.fori_loop(0, SP, step, 0)

    def b_chunk(n, carry):
        s, r = n // ROW_CHUNKS, n % ROW_CHUNKS
        norm_chunk(hid, b_all, 1, n * tile, 2 * s * tokens + r * tile)
        copy(
            s_b + n,
            b_all.at[rows(2 * s * tokens + r * tile, tile)],
            b_all.at[rows((2 * s + 1) * tokens + r * tile, tile)],
            to[1],
        ).start()
        return carry

    def gate_phase(w_buf):
        def w_load(slot, start, size):
            mine = [
                load(4 * slot + t, (wg, wu)[t].at[:, cols(me * feat + start, size)], w_buf.at[slot, 0:half, t * size : (t + 1) * size])
                for t in range(2)
            ]
            other = [
                load(4 * slot + 2 + t, gu_rem.at[t, :, cols(start, size)], w_buf.at[slot, half:dim, t * size : (t + 1) * size])
                for t in range(2)
            ]
            return mine, other

        def run(c, side, slot, start, size):
            def body(b_ref, o_ref):
                parts = [dot(b_ref[...], w_buf[slot, :, n * NB : (n + 1) * NB]) for n in range(2 * size // NB)]
                both = [p[:, lo : lo + 128] for p in parts for lo in (0, 128)]
                n = size // 128
                for i in range(n):
                    o_ref[:, i * 128 : (i + 1) * 128] = (jax.nn.silu(both[i]) * both[n + i]).astype(BF16)

            n_t = 2 * ROW_CHUNKS
            pltpu.emit_pipeline(
                body,
                grid=(n_t,),
                in_specs=[pl.BlockSpec((tile, dim), lambda t: (side * n_t + t, 0))],
                out_specs=[pl.BlockSpec((tile, size), lambda t: (side * n_t + t, 0))],
            )(b_all, u_own.at[:, cols(start, size)])

            @pl.when(side == 0)
            def _():
                u_copy(c, 1, start, size).start()

            @pl.when(side == 1)
            def _():
                u_copy(c, 2, start, size).start()
                u_copy(c, 3, start, size).start()

        def chunk(c, slot, start, size, prefetch):
            mine, other = w_load(slot, start, size)
            for t in range(2):
                gu_copy(c, t, start, size).wait_recv()
            for d in other:
                d.start()
            for d in mine + other:
                d.wait()
            prefetch()

            def sides(t, carry):
                side = 1 - t

                @pl.when(c == 0)
                def _():
                    for r in range(ROW_CHUNKS):
                        n = side * ROW_CHUNKS + r
                        copy(
                            s_b + n,
                            b_all.at[rows(2 * side * tokens + r * tile, tile)],
                            b_all.at[rows((2 * side + 1) * tokens + r * tile, tile)],
                            to[1],
                        ).wait_recv()

                run(c, side, slot, start, size)
                return carry

            lax.fori_loop(0, 2, sides, 0)

        for d in w_load(0, 0, GATE_COLS)[0]:
            d.start()

        def full(c, carry):
            def prefetch():
                @pl.when(c + 1 < FULL_CHUNKS)
                def _():
                    for d in w_load((c + 1) % 2, (c + 1) * GATE_COLS, GATE_COLS)[0]:
                        d.start()

                @pl.when(c + 1 == FULL_CHUNKS)
                def _():
                    for d in w_load((c + 1) % 2, starts[FULL_CHUNKS], sizes[FULL_CHUNKS])[0]:
                        d.start()

            chunk(c, c % 2, c * GATE_COLS, GATE_COLS, prefetch)
            return carry

        lax.fori_loop(0, FULL_CHUNKS, full, 0)
        for c in range(FULL_CHUNKS, chunks):

            def prefetch(c=c):
                if c + 1 < chunks:
                    for d in w_load((c + 1) % 2, starts[c + 1], sizes[c + 1])[0]:
                        d.start()

            chunk(c, c % 2, starts[c], sizes[c], prefetch)

    def down_phase(u_buf, w_mine, w_other, h_buf, acc_buf, o_buf):
        total = SP * down_chunks
        pieces = DOWN_PARTS * down_chunks
        band = tokens // 2

        def pass_y(m):
            @pl.when(m < pieces)
            def _():
                wd_copy(m, 0).wait_recv()
                wd_copy(m, 2).start()
                wd_copy(m, 1).start()

        def pass_x(m):
            wd_copy(m, 2).wait_recv()
            wd_copy(m, 3).start()

        def u_load(k):
            sp = sp_of(k)
            at = ((sp // 2 + y) % 2) * half_feat + (sp % 2) * feat
            return load(k, (u_got if k else u_own).at[pl.ds(k * tokens, tokens)], u_buf.at[:, cols(at, feat)])

        def out_cols(n):
            return cols(sp_of(n % 4) * quarter + (n // 4) * DOWN_COLS, DOWN_COLS)

        def fetch(n):
            slot = n % 2
            here = out_cols(n)
            return [load(4 + 2 * slot, wd.at[:, here], w_mine.at[slot]), load(5 + 2 * slot, hid.at[0:tokens, here], h_buf.at[slot])]

        def store(n):
            return load(8 + n % 2, o_buf.at[n % 2], out.at[:, out_cols(n)])

        for d in fetch(0):
            d.start()
        u_load(0).start()
        for k in (1, 2, 3):
            for c in range(chunks):
                u_copy(c, k, starts[c], sizes[c]).wait_recv()
            u_load(k).start()
        pass_y(0)
        pass_y(1)
        for k in range(SP):
            u_load(k).wait()

        def step(i, carry):
            n = i - 2
            c, k = n // 4, n % 4

            @pl.when((n >= 0) & (k == 0))
            def _():
                pass_x(4 * c)
                pass_y(4 * c + 2)
                pass_y(4 * c + 3)

            @pl.when((n >= 0) & (k == 1))
            def _():
                pass_x(4 * c + 1)
                pass_x(4 * c + 2)

            @pl.when((n >= 0) & (k == 2))
            def _():
                pass_y(4 * c + 4)
                pass_x(4 * c + 3)

            @pl.when((n >= 0) & (k == 3))
            def _():
                pass_y(4 * c + 5)

            for side in (1, 3):

                @pl.when((n >= 0) & (k == side))
                def _():
                    for p in range(DOWN_PARTS):
                        wd_copy(DOWN_PARTS * c + p, side).wait_recv()

            def other_load():
                return load(10, wd_rem.at[k, :, cols(c * DOWN_COLS, DOWN_COLS)], w_other)

            @pl.when(n >= 0)
            def _():
                other_load().start()

            @pl.when(i + 1 < total)
            def _():
                for d in fetch(i + 1):
                    d.start()

            @pl.when(i < total)
            def _():
                for d in fetch(i):
                    d.wait()

                def mine(t, c2):
                    m = rows(t * band, band)
                    acc_buf[i % 3, m] = h_buf[i % 2, m].astype(F32) + dot(u_buf[m, 0:half_feat], w_mine[i % 2])
                    return c2

                lax.fori_loop(0, 2, mine, 0)

            @pl.when(n >= 0)
            def _():
                other_load().wait()

                @pl.when(n >= 2)
                def _():
                    store(n - 2).wait()

                def other(t, c2):
                    m = rows(t * band, band)
                    o_buf[n % 2, m] = (acc_buf[n % 3, m] + dot(u_buf[m, half_feat:], w_other[...])).astype(BF16)
                    return c2

                lax.fori_loop(0, 2, other, 0)
                store(n).start()

            return carry

        lax.fori_loop(0, total + 2, step, 0)
        for n in (total - 2, total - 1):
            store(n).wait()

    lax.fori_loop(0, ROW_CHUNKS, own_a, 0)
    pl.run_scoped(attention, pltpu.VMEM((dim, 2 * eighth), BF16), pltpu.VMEM((dim, eighth), BF16))
    pl.run_scoped(out_phase, pltpu.VMEM((2, dim, quarter), BF16), pltpu.VMEM((2 * num_rows, shard_len, dim), BF16))
    lax.fori_loop(0, 2 * ROW_CHUNKS, b_chunk, 0)
    pl.run_scoped(gate_phase, pltpu.VMEM((2, dim, 2 * GATE_COLS), BF16))
    pl.run_scoped(
        down_phase,
        pltpu.VMEM((tokens, 2 * half_feat), BF16),
        pltpu.VMEM((2, half_feat, DOWN_COLS), BF16),
        pltpu.VMEM((half_feat, DOWN_COLS), BF16),
        pltpu.VMEM((2, tokens, DOWN_COLS), BF16),
        pltpu.VMEM((3, tokens, DOWN_COLS), F32),
        pltpu.VMEM((2, tokens, DOWN_COLS), BF16),
    )

    gain_copy.wait_send()
    for h in range(2):
        for j in range(3):
            qkv_copy(j, h).wait_send()
    for k in range(SP):
        wo_copy(k).wait_send()
    for c in range(chunks):
        for t in range(2):
            gu_copy(c, t, starts[c], sizes[c]).wait_send()
        for k in (1, 2, 3):
            u_copy(c, k, starts[c], sizes[c]).wait_send()
    for r in range(ROW_CHUNKS):
        x_copy(r).wait_send()
        for piece in (0, 2):
            act_copy(s_a, a_all, piece, r).wait_send()
            act_copy(s_b, b_all, piece, r).wait_send()

        def o_sent(h, carry):
            for k in (1, 2, 3):
                for s in range(2):
                    o_copy(h, r, k, s).wait_send()
            return carry

        lax.fori_loop(0, 2, o_sent, 0)

    def wd_sent(m, carry):
        for k in range(SP):
            wd_copy(m, k).wait_send()
        return carry

    lax.fori_loop(0, DOWN_PARTS * down_chunks, wd_sent, 0)


def tables(shard_len):
    inv_freq = np.exp(np.arange(HEAD_DIM // 2, dtype=np.float32) * np.float32(-2.0 * math.log(ROPE_THETA) / HEAD_DIM))
    pos = np.arange(shard_len)[None, :] * SP + np.arange(SP)[:, None]
    angles = (pos.astype(np.float32)[..., None] * inv_freq.astype(np.float32)).astype(np.float64)
    cos, sin = np.cos(angles), np.sin(angles)
    return (
        np.concatenate([cos, cos], axis=-1).astype(np.float32),
        np.concatenate([-sin, sin], axis=-1).astype(np.float32),
    )


def local_layer(x_loc, norm_attn, w_query, w_key, w_value, w_out, norm_mlp, w_gate, w_up, w_down):
    num_rows, shard_len, dim = x_loc.shape
    tokens = num_rows * shard_len
    half, quarter, eighth = dim // 2, dim // 4, dim // 8
    half_feat = w_down.shape[0]
    feat = half_feat // 2
    gain = jnp.zeros((8, half), F32).at[0].set(norm_attn.astype(F32)).at[1].set(norm_mlp.astype(F32))
    cos, sin = tables(shard_len)

    def buf(*shape):
        return jax.ShapeDtypeStruct(shape, BF16)

    shapes = [
        buf(tokens, dim),
        buf(tokens, dim),
        buf(SP * tokens, dim),
        buf(6, half, eighth),
        buf(SP, half, quarter),
        buf(2, half, feat),
        buf(SP, half_feat, quarter),
        buf(6 * SP, num_rows, shard_len, eighth),
        buf(2 * SP, num_rows, shard_len, eighth),
        buf(12, num_rows, shard_len, eighth),
        buf(2 * tokens, dim),
        buf(SP * tokens, dim),
        buf(SP * tokens, feat),
        buf(SP * tokens, feat),
    ]
    chunks = FULL_CHUNKS + 2
    copies = 1 + 6 + 4 + 2 * chunks + 4 * DOWN_PARTS * (quarter // DOWN_COLS) + 17 * ROW_CHUNKS + 3 * chunks
    outs = pl.pallas_call(
        layer_kernel,
        out_shape=shapes,
        in_specs=[ANY, VM] + [ANY] * 9,
        out_specs=[ANY] * len(shapes),
        scratch_shapes=[
            pltpu.VMEM((8, half), F32),
            pltpu.VMEM((SP, shard_len, HEAD_DIM), F32),
            pltpu.VMEM((SP, shard_len, HEAD_DIM), F32),
            pltpu.SemaphoreType.DMA((copies,)),
            pltpu.SemaphoreType.DMA((copies,)),
            pltpu.SemaphoreType.DMA((20,)),
        ],
        compiler_params=pltpu.CompilerParams(collective_id=0, has_side_effects=True, vmem_limit_bytes=67043328),
        name="decoder_layer",
    )(x_loc.reshape(tokens, dim), gain, w_query, w_key, w_value, w_out, w_gate, w_up, w_down, jnp.asarray(cos), jnp.asarray(sin))
    return outs[0].reshape(x_loc.shape)


def solution(mesh):
    row_spec = P(("dp", "fsdp"), "sp", None)
    weight_spec = P("fsdp", None)
    gain_spec = P("fsdp")
    in_specs = (row_spec, gain_spec, weight_spec, weight_spec, weight_spec, weight_spec, gain_spec, weight_spec, weight_spec, weight_spec)
    fn = jax.shard_map(local_layer, mesh=mesh, in_specs=in_specs, out_specs=row_spec, check_vma=False)

    def run(*args):
        with jax.sharding.use_abstract_mesh(mesh.abstract_mesh):
            return fn(*args)

    return run
```

time: 7970 us -> 1780 us (0.22)
  waiting for transfers between devices: 6750 us -> 0 us
  Pallas kernels: 0 us -> 1760 us
  matrix products: 936 us -> 0 us
  other arithmetic: 148 us -> 0.65 us
  local copies, waits for them, and re-layouts: 114 us -> 12.9 us
    all_gather x9 -> x0, waiting for transfers between devices: 6740 us -> none  [the longest x7 6400 us: gather_weight(): return lax.all_gather(weight_shard, 'fsdp', axis=0, tiled=True)]
    pallas_call x0 -> x1, Pallas kernels: none -> 1760 us  [local_layer(): pl.pallas_call(layer_kernel, out_shape=shapes, in_specs=[ANY, VM] + [ANY]...]
    dot_general x9 -> x0, matrix products: 936 us -> none  [the longest x1 186 us: local_layer(): jnp.dot(normed_mlp, gather_weight(w_up), preferred_element_type=jnp.float32)]
  transfers between devices with their start and end apart: 9 -> 0, of which waited for: 9 -> 0; matrix products, arithmetic and copies ran while one was open for 13% -> 0% of each run, Pallas kernels for 0% -> 0%
where the time goes in v2:
time: 1780 us; the launch traced here: 1770 us
  Pallas kernels  1760 us (99%)
    pallas_call x1, Pallas kernels, local_layer(): pl.pallas_call(layer_kernel, out_shape=shapes, in_specs=[ANY, VM] + [ANY]...  1760 us

profile of v2, /device:TPU:0, one launch (start us, length us, event | category | flops | bytes accessed | tf_op | source)
XLA Modules:
  0.0 1773.7 jit_solution(11453578778988028781)
XLA Ops:
  0.0 0.7 reshape.61
  0.7 0.7 reshape.64
  1.4 0.6 pad_convert_fusion
  2.0 1.6 scatter.14.gain
  3.6 1760.1 %decoder_layer.1 = (bf16[1152,5120]{1,0:T(8,128)(2,1)}, bf16[1152,5120]{1,0:T(8,128)(2,1)}, bf16[4608,5120]{1,0:T(8,128)(2,1)}, bf16[6,2560,640]{2,1,0:T(8,128)(...) custom-call(bf16[1152,5120]{1,0:T(8,128)(2,1)} %bitcast.3, ...), custom_call_target="tpu_custom_call" | custom-call | tf_op jit(solution)/shard_map/decoder_layer/pallas_call | solution.py:731
  1763.7 10.0 copy.15

commit v3 on v2

--- a/solution.py
+++ b/solution.py
@@ -26,6 +26,7 @@
 FULL_CHUNKS = 8
 DOWN_COLS = 256
 DOWN_PARTS = 4
+LAST_PARTS = 9
 ROW_CHUNKS = 3
 
 
@@ -34,9 +35,9 @@
 
 
 def layer_kernel(
-    x, gain, wq, wk, wv, wo, wg, wu, wd, cos, sin,
-    out, x_got, a_all, qkv_rem, wo_rem, gu_rem, wd_rem, qkv, o_own, o_got, hid, b_all, u_own, u_got,
-    gain_rem, cos_buf, sin_buf, send_sem, recv_sem, load_sem,
+    x, gain_attn, gain_mlp, wq, wk, wv, wo, wg, wu, wd, cos, sin,
+    out, rem_attn, rem_mlp, x_got, a_all, qkv_rem, wo_rem, gu_rem, wd_rem, qkv, o_own, o_got, hid, b_all, u_own, u_got,
+    gain_a, rem_a, gain_m, rem_m, cos_buf, sin_buf, send_sem, recv_sem, load_sem,
 ):
     tokens, dim = x.shape
     num_rows, shard_len = o_own.shape[1], o_own.shape[2]
@@ -46,7 +47,7 @@
     tile = tokens // ROW_CHUNKS
     tile_rows = num_rows // ROW_CHUNKS
     down_chunks = quarter // DOWN_COLS
-    part_rows = half_feat // DOWN_PARTS
+    part_rows, last_rows = half_feat // DOWN_PARTS, half_feat // LAST_PARTS
     heads = eighth // HEAD_DIM
     rest = feat - FULL_CHUNKS * GATE_COLS
     sizes = [GATE_COLS] * FULL_CHUNKS + [rest - 128, 128]
@@ -75,8 +76,8 @@
         used[0] += n
         return used[0] - n
 
-    s_gain, s_qkv, s_wo, s_gu = slots(1), slots(6), slots(4), slots(2 * chunks)
-    s_wd = slots(4 * DOWN_PARTS * down_chunks)
+    s_gain, s_qkv, s_wo, s_gu = slots(2), slots(6), slots(4), slots(2 * chunks)
+    s_wd, s_wl = slots(4 * DOWN_PARTS * (down_chunks - 1)), slots(4 * LAST_PARTS)
     s_x, s_a, s_b = slots(ROW_CHUNKS), slots(2 * ROW_CHUNKS), slots(2 * ROW_CHUNKS)
     s_o, s_u = slots(12 * ROW_CHUNKS), slots(3 * chunks)
 
@@ -97,7 +98,7 @@
         here = rows(r * tile, tile)
         return copy(s_x + r, x.at[here], x_got.at[here], to[2])
 
-    gain_copy = copy(s_gain, gain, gain_rem, to_y)
+    gain_copies = [copy(s_gain, gain_attn, rem_attn, to_y), copy(s_gain + 1, gain_mlp, rem_mlp, to_y)]
 
     def qkv_copy(j, h):
         part = (1 - y + h) % 2
@@ -119,6 +120,15 @@
             return copy(s_wd + 4 * m, wd.at[part, cols(me * quarter + col, DOWN_COLS)], wd_rem.at[0, part, cols(col, DOWN_COLS)], to_y)
         here = (part, cols(col, DOWN_COLS))
         return copy(s_wd + 4 * m + k, wd_rem.at[(2 if k == 3 else 0, *here)], wd_rem.at[(k, *here)], to[2] if k == 2 else to[1])
+
+    def wl_copy(p, k):
+        last = quarter - DOWN_COLS
+        part = rows(p * last_rows, last_rows)
+        if k == 0:
+            src = wd.at[part, cols(me * quarter + last, DOWN_COLS)]
+            return copy(s_wl + 4 * p, src, wd_rem.at[0, part, cols(last, DOWN_COLS)], to_y)
+        here = (part, cols(last, DOWN_COLS))
+        return copy(s_wl + 4 * p + k, wd_rem.at[(2 if k == 3 else 0, *here)], wd_rem.at[(k, *here)], to[2] if k == 2 else to[1])
 
     def act_copy(base, ref, piece, r):
         return copy(
@@ -144,7 +154,8 @@
 
     for r in range(ROW_CHUNKS):
         x_copy(r).start()
-    gain_copy.start()
+    for d in gain_copies:
+        d.start()
     for h in range(2):
         for j in range(3):
             qkv_copy(j, h).start()
@@ -152,19 +163,25 @@
     for c in range(chunks):
         for t in range(2):
             gu_copy(c, t, starts[c], sizes[c]).start()
-    for m in range(DOWN_PARTS * down_chunks):
+    for m in range(DOWN_PARTS * (down_chunks - 1)):
         wd_copy(m, 0).start()
-    tabs = [load(0, cos, cos_buf), load(1, sin, sin_buf)]
+    for p in range(LAST_PARTS):
+        wl_copy(p, 0).start()
+    tabs = [load(0, cos, cos_buf), load(1, sin, sin_buf), load(2, gain_attn, gain_a), load(3, gain_mlp, gain_m)]
     for d in tabs:
+        d.start()
+    for d in gain_copies:
+        d.wait_recv()
+    tabs += [load(4, rem_attn, rem_a), load(5, rem_mlp, rem_m)]
+    for d in tabs[4:]:
         d.start()
     for d in tabs:
         d.wait()
-    gain_copy.wait_recv()
 
     def norm_chunk(src, dst, which, src_row, dst_row):
         n = tile // 3
-        gm = gain[which : which + 1, :]
-        go = gain_rem[which : which + 1, :]
+        gm = (gain_a, gain_m)[which][...].astype(F32).reshape(1, half)
+        go = (rem_a, rem_m)[which][...].astype(F32).reshape(1, half)
 
         def body(in_ref, out_ref):
             def sub(s, carry):
@@ -520,7 +537,8 @@
 
     def down_phase(u_buf, w_mine, w_other, h_buf, acc_buf, o_buf):
         total = SP * down_chunks
-        pieces = DOWN_PARTS * down_chunks
+        main = total - SP
+        pieces = DOWN_PARTS * (down_chunks - 1)
         band = tokens // 2
 
         def pass_y(m):
@@ -533,6 +551,11 @@
         def pass_x(m):
             wd_copy(m, 2).wait_recv()
             wd_copy(m, 3).start()
+
+        def last_y(p):
+            wl_copy(p, 0).wait_recv()
+            wl_copy(p, 2).start()
+            wl_copy(p, 1).start()
 
         def u_load(k):
             sp = sp_of(k)
@@ -540,7 +563,7 @@
             return load(k, (u_got if k else u_own).at[pl.ds(k * tokens, tokens)], u_buf.at[:, cols(at, feat)])
 
         def out_cols(n):
-            return cols(sp_of(n % 4) * quarter + (n // 4) * DOWN_COLS, DOWN_COLS)
+            return cols(sp_of(n % SP) * quarter + (n // SP) * DOWN_COLS, DOWN_COLS)
 
         def fetch(n):
             slot = n % 2
@@ -548,7 +571,23 @@
             return [load(4 + 2 * slot, wd.at[:, here], w_mine.at[slot]), load(5 + 2 * slot, hid.at[0:tokens, here], h_buf.at[slot])]
 
         def store(n):
-            return load(8 + n % 2, o_buf.at[n % 2], out.at[:, out_cols(n)])
+            return load(8 + n % SP, o_buf.at[n % SP], out.at[:, out_cols(n)])
+
+        def mine(n):
+            @pl.when(n + 1 < total)
+            def _():
+                for d in fetch(n + 1):
+                    d.start()
+
+            for d in fetch(n):
+                d.wait()
+
+            def part(t, carry):
+                m = rows(t * band, band)
+                acc_buf[n % SP, m] = h_buf[n % 2, m].astype(F32) + dot(u_buf[m, 0:half_feat], w_mine[n % 2])
+                return carry
+
+            lax.fori_loop(0, 2, part, 0)
 
         for d in fetch(0):
             d.start()
@@ -564,7 +603,7 @@
 
         def step(i, carry):
             n = i - 2
-            c, k = n // 4, n % 4
+            c, k = n // SP, n % SP
 
             @pl.when((n >= 0) & (k == 0))
             def _():
@@ -585,6 +624,16 @@
             @pl.when((n >= 0) & (k == 3))
             def _():
                 pass_y(4 * c + 5)
+
+            @pl.when(n == main - 2)
+            def _():
+                last_y(0)
+                last_y(1)
+
+            @pl.when(n == main - 1)
+            def _():
+                last_y(2)
+                last_y(3)
 
             for side in (1, 3):
 
@@ -594,50 +643,108 @@
                         wd_copy(DOWN_PARTS * c + p, side).wait_recv()
 
             def other_load():
-                return load(10, wd_rem.at[k, :, cols(c * DOWN_COLS, DOWN_COLS)], w_other)
+                return load(12, wd_rem.at[k, :, cols(c * DOWN_COLS, DOWN_COLS)], w_other)
 
             @pl.when(n >= 0)
             def _():
                 other_load().start()
 
-            @pl.when(i + 1 < total)
-            def _():
-                for d in fetch(i + 1):
-                    d.start()
-
-            @pl.when(i < total)
-            def _():
-                for d in fetch(i):
-                    d.wait()
-
-                def mine(t, c2):
+            mine(i)
+
+            @pl.when(n >= 0)
+            def _():
+                other_load().wait()
+
+                @pl.when(n >= SP)
+                def _():
+                    store(n - SP).wait()
+
+                def part(t, c2):
                     m = rows(t * band, band)
-                    acc_buf[i % 3, m] = h_buf[i % 2, m].astype(F32) + dot(u_buf[m, 0:half_feat], w_mine[i % 2])
+                    o_buf[n % SP, m] = (acc_buf[n % SP, m] + dot(u_buf[m, half_feat:], w_other[...])).astype(BF16)
                     return c2
 
-                lax.fori_loop(0, 2, mine, 0)
-
-            @pl.when(n >= 0)
-            def _():
-                other_load().wait()
-
-                @pl.when(n >= 2)
-                def _():
-                    store(n - 2).wait()
-
-                def other(t, c2):
-                    m = rows(t * band, band)
-                    o_buf[n % 2, m] = (acc_buf[n % 3, m] + dot(u_buf[m, half_feat:], w_other[...])).astype(BF16)
-                    return c2
-
-                lax.fori_loop(0, 2, other, 0)
+                lax.fori_loop(0, 2, part, 0)
                 store(n).start()
 
             return carry
 
-        lax.fori_loop(0, total + 2, step, 0)
-        for n in (total - 2, total - 1):
-            store(n).wait()
+        lax.fori_loop(0, main + 2, step, 0)
+        last_y(4)
+
+        def rest_mine(n, carry):
+            mine(n)
+
+            @pl.when(n == main + 2)
+            def _():
+                last_y(5)
+
+            return carry
+
+        lax.fori_loop(main + 2, total, rest_mine, 0)
+        for k in range(SP):
+            store(main - SP + k).wait()
+
+        def piece_load(k, p):
+            at = rows((2 * k + p % 2) * last_rows, last_rows)
+            return load(2 * k + p % 2, wd_rem.at[k, rows(p * last_rows, last_rows), cols(quarter - DOWN_COLS, DOWN_COLS)], w_other.at[at])
+
+        def piece_dot(k, p):
+            piece_load(k, p).wait()
+            at = rows((2 * k + p % 2) * last_rows, last_rows)
+            acc_buf[k] = acc_buf[k] + dot(u_buf[:, cols(half_feat + p * last_rows, last_rows)], w_other[at])
+
+        def finish(k):
+            o_buf[k] = acc_buf[k].astype(BF16)
+            store(main + k).start()
+
+        def first_two(p):
+            wl_copy(p, 1).wait_recv()
+            for k in (0, 1):
+                piece_load(k, p).start()
+
+        first_two(0)
+
+        def last_step(p, carry):
+            @pl.when(p + 6 < LAST_PARTS)
+            def _():
+                last_y(p + 6)
+
+            piece_dot(0, p)
+            piece_dot(1, p)
+
+            @pl.when(p == LAST_PARTS - 1)
+            def _():
+                finish(0)
+                finish(1)
+
+            wl_copy(p, 2).wait_recv()
+            wl_copy(p, 3).start()
+            piece_load(2, p).start()
+
+            @pl.when(p + 1 < LAST_PARTS)
+            def _():
+                first_two(p + 1)
+
+            @pl.when(p > 0)
+            def _():
+                piece_dot(3, p - 1)
+
+            piece_dot(2, p)
+
+            @pl.when(p == LAST_PARTS - 1)
+            def _():
+                finish(2)
+
+            wl_copy(p, 3).wait_recv()
+            piece_load(3, p).start()
+            return carry
+
+        lax.fori_loop(0, LAST_PARTS, last_step, 0)
+        piece_dot(3, LAST_PARTS - 1)
+        finish(3)
+        for k in range(SP):
+            store(main + k).wait()
 
     lax.fori_loop(0, ROW_CHUNKS, own_a, 0)
     pl.run_scoped(attention, pltpu.VMEM((dim, 2 * eighth), BF16), pltpu.VMEM((dim, eighth), BF16))
@@ -650,11 +757,12 @@
         pltpu.VMEM((2, half_feat, DOWN_COLS), BF16),
         pltpu.VMEM((half_feat, DOWN_COLS), BF16),
         pltpu.VMEM((2, tokens, DOWN_COLS), BF16),
-        pltpu.VMEM((3, tokens, DOWN_COLS), F32),
-        pltpu.VMEM((2, tokens, DOWN_COLS), BF16),
+        pltpu.VMEM((SP, tokens, DOWN_COLS), F32),
+        pltpu.VMEM((SP, tokens, DOWN_COLS), BF16),
     )
 
-    gain_copy.wait_send()
+    for d in gain_copies:
+        d.wait_send()
     for h in range(2):
         for j in range(3):
             qkv_copy(j, h).wait_send()
@@ -684,7 +792,14 @@
             wd_copy(m, k).wait_send()
         return carry
 
-    lax.fori_loop(0, DOWN_PARTS * down_chunks, wd_sent, 0)
+    lax.fori_loop(0, DOWN_PARTS * (down_chunks - 1), wd_sent, 0)
+
+    def wl_sent(p, carry):
+        for k in range(SP):
+            wl_copy(p, k).wait_send()
+        return carry
+
+    lax.fori_loop(0, LAST_PARTS, wl_sent, 0)
 
 
 def tables(shard_len):
@@ -704,7 +819,6 @@
     half, quarter, eighth = dim // 2, dim // 4, dim // 8
     half_feat = w_down.shape[0]
     feat = half_feat // 2
-    gain = jnp.zeros((8, half), F32).at[0].set(norm_attn.astype(F32)).at[1].set(norm_mlp.astype(F32))
     cos, sin = tables(shard_len)
 
     def buf(*shape):
@@ -712,6 +826,8 @@
 
     shapes = [
         buf(tokens, dim),
+        buf(half),
+        buf(half),
         buf(tokens, dim),
         buf(SP * tokens, dim),
         buf(6, half, eighth),
@@ -727,14 +843,14 @@
         buf(SP * tokens, feat),
     ]
     chunks = FULL_CHUNKS + 2
-    copies = 1 + 6 + 4 + 2 * chunks + 4 * DOWN_PARTS * (quarter // DOWN_COLS) + 17 * ROW_CHUNKS + 3 * chunks
+    copies = 2 + 6 + 4 + 2 * chunks + 4 * DOWN_PARTS * (quarter // DOWN_COLS - 1) + 4 * LAST_PARTS + 17 * ROW_CHUNKS + 3 * chunks
     outs = pl.pallas_call(
         layer_kernel,
         out_shape=shapes,
-        in_specs=[ANY, VM] + [ANY] * 9,
+        in_specs=[ANY] * 12,
         out_specs=[ANY] * len(shapes),
         scratch_shapes=[
-            pltpu.VMEM((8, half), F32),
+            *[pltpu.VMEM((half,), BF16)] * 4,
             pltpu.VMEM((SP, shard_len, HEAD_DIM), F32),
             pltpu.VMEM((SP, shard_len, HEAD_DIM), F32),
             pltpu.SemaphoreType.DMA((copies,)),
@@ -743,7 +859,7 @@
         ],
         compiler_params=pltpu.CompilerParams(collective_id=0, has_side_effects=True, vmem_limit_bytes=67043328),
         name="decoder_layer",
-    )(x_loc.reshape(tokens, dim), gain, w_query, w_key, w_value, w_out, w_gate, w_up, w_down, jnp.asarray(cos), jnp.asarray(sin))
+    )(x_loc.reshape(tokens, dim), norm_attn, norm_mlp, w_query, w_key, w_value, w_out, w_gate, w_up, w_down, jnp.asarray(cos), jnp.asarray(sin))
     return outs[0].reshape(x_loc.shape)
 
 

time: 1780 us -> 1760 us (0.989)
  no operation moved by 1% of the time
where the time goes in v3:
time: 1760 us
  Pallas kernels  1750 us (99%)
    pallas_call x1, Pallas kernels, local_layer(): pl.pallas_call(layer_kernel, out_shape=shapes, in_specs=[ANY] * 12, out_s...  1750 us

profile of v3, /device:TPU:0, one launch (start us, length us, event | category | flops | bytes accessed | tf_op | source)
XLA Modules:
  0.0 1761.6 jit_solution(11430227420153090120)
XLA Ops:
  0.0 1751.6 %decoder_layer.1 = (bf16[1152,5120]{1,0:T(8,128)(2,1)}, bf16[2560]{0:T(1024)(128)(2,1)}, bf16[2560]{0:T(1024)(128)(2,1)}, bf16[1152,5120]{1,0:T(8,128)(2,1)}, bf...) custom-call(bf16[1152,5120]{1,0:T(8,128)(2,1)} %bitcast.3, ...), custom_call_target="tpu_custom_call" | custom-call | tf_op jit(solution)/shard_map/decoder_layer/pallas_call | solution.py:847
  1751.6 10.0 copy.14

commit v4 on v3

--- a/solution.py
+++ b/solution.py
@@ -25,8 +25,7 @@
 GATE_COLS = 384
 FULL_CHUNKS = 8
 DOWN_COLS = 256
-DOWN_PARTS = 4
-LAST_PARTS = 9
+DOWN_PARTS = 9
 ROW_CHUNKS = 3
 
 
@@ -47,7 +46,7 @@
     tile = tokens // ROW_CHUNKS
     tile_rows = num_rows // ROW_CHUNKS
     down_chunks = quarter // DOWN_COLS
-    part_rows, last_rows = half_feat // DOWN_PARTS, half_feat // LAST_PARTS
+    part_rows = half_feat // DOWN_PARTS
     heads = eighth // HEAD_DIM
     rest = feat - FULL_CHUNKS * GATE_COLS
     sizes = [GATE_COLS] * FULL_CHUNKS + [rest - 128, 128]
@@ -77,7 +76,7 @@
         return used[0] - n
 
     s_gain, s_qkv, s_wo, s_gu = slots(2), slots(6), slots(4), slots(2 * chunks)
-    s_wd, s_wl = slots(4 * DOWN_PARTS * (down_chunks - 1)), slots(4 * LAST_PARTS)
+    s_wd = slots(4 * DOWN_PARTS * down_chunks)
     s_x, s_a, s_b = slots(ROW_CHUNKS), slots(2 * ROW_CHUNKS), slots(2 * ROW_CHUNKS)
     s_o, s_u = slots(12 * ROW_CHUNKS), slots(3 * chunks)
 
@@ -120,15 +119,6 @@
             return copy(s_wd + 4 * m, wd.at[part, cols(me * quarter + col, DOWN_COLS)], wd_rem.at[0, part, cols(col, DOWN_COLS)], to_y)
         here = (part, cols(col, DOWN_COLS))
         return copy(s_wd + 4 * m + k, wd_rem.at[(2 if k == 3 else 0, *here)], wd_rem.at[(k, *here)], to[2] if k == 2 else to[1])
-
-    def wl_copy(p, k):
-        last = quarter - DOWN_COLS
-        part = rows(p * last_rows, last_rows)
-        if k == 0:
-            src = wd.at[part, cols(me * quarter + last, DOWN_COLS)]
-            return copy(s_wl + 4 * p, src, wd_rem.at[0, part, cols(last, DOWN_COLS)], to_y)
-        here = (part, cols(last, DOWN_COLS))
-        return copy(s_wl + 4 * p + k, wd_rem.at[(2 if k == 3 else 0, *here)], wd_rem.at[(k, *here)], to[2] if k == 2 else to[1])
 
     def act_copy(base, ref, piece, r):
         return copy(
@@ -163,10 +153,8 @@
     for c in range(chunks):
         for t in range(2):
             gu_copy(c, t, starts[c], sizes[c]).start()
-    for m in range(DOWN_PARTS * (down_chunks - 1)):
+    for m in range(DOWN_PARTS * down_chunks):
         wd_copy(m, 0).start()
-    for p in range(LAST_PARTS):
-        wl_copy(p, 0).start()
     tabs = [load(0, cos, cos_buf), load(1, sin, sin_buf), load(2, gain_attn, gain_a), load(3, gain_mlp, gain_m)]
     for d in tabs:
         d.start()
@@ -538,24 +526,20 @@
     def down_phase(u_buf, w_mine, w_other, h_buf, acc_buf, o_buf):
         total = SP * down_chunks
         main = total - SP
-        pieces = DOWN_PARTS * (down_chunks - 1)
+        pieces = DOWN_PARTS * down_chunks
+        last = pieces - DOWN_PARTS
         band = tokens // 2
 
-        def pass_y(m):
-            @pl.when(m < pieces)
-            def _():
+        def pass_y(*ms):
+            for m in ms:
                 wd_copy(m, 0).wait_recv()
                 wd_copy(m, 2).start()
                 wd_copy(m, 1).start()
 
-        def pass_x(m):
-            wd_copy(m, 2).wait_recv()
-            wd_copy(m, 3).start()
-
-        def last_y(p):
-            wl_copy(p, 0).wait_recv()
-            wl_copy(p, 2).start()
-            wl_copy(p, 1).start()
+        def pass_x(*ms):
+            for m in ms:
+                wd_copy(m, 2).wait_recv()
+                wd_copy(m, 3).start()
 
         def u_load(k):
             sp = sp_of(k)
@@ -592,64 +576,77 @@
         for d in fetch(0):
             d.start()
         u_load(0).start()
+        pass_y(0, 1, 2)
         for k in (1, 2, 3):
             for c in range(chunks):
                 u_copy(c, k, starts[c], sizes[c]).wait_recv()
             u_load(k).start()
-        pass_y(0)
-        pass_y(1)
+        pass_y(3)
+        pass_x(0)
         for k in range(SP):
             u_load(k).wait()
 
         def step(i, carry):
             n = i - 2
             c, k = n // SP, n % SP
-
-            @pl.when((n >= 0) & (k == 0))
-            def _():
-                pass_x(4 * c)
-                pass_y(4 * c + 2)
-                pass_y(4 * c + 3)
-
-            @pl.when((n >= 0) & (k == 1))
-            def _():
-                pass_x(4 * c + 1)
-                pass_x(4 * c + 2)
-
-            @pl.when((n >= 0) & (k == 2))
-            def _():
-                pass_y(4 * c + 4)
-                pass_x(4 * c + 3)
-
-            @pl.when((n >= 0) & (k == 3))
-            def _():
-                pass_y(4 * c + 5)
-
-            @pl.when(n == main - 2)
-            def _():
-                last_y(0)
-                last_y(1)
-
-            @pl.when(n == main - 1)
-            def _():
-                last_y(2)
-                last_y(3)
-
-            for side in (1, 3):
-
-                @pl.when((n >= 0) & (k == side))
-                def _():
-                    for p in range(DOWN_PARTS):
-                        wd_copy(DOWN_PARTS * c + p, side).wait_recv()
+            j = DOWN_PARTS * c
 
             def other_load():
                 return load(12, wd_rem.at[k, :, cols(c * DOWN_COLS, DOWN_COLS)], w_other)
 
-            @pl.when(n >= 0)
+            def arrived(side):
+                for p in range(DOWN_PARTS):
+                    wd_copy(j + p, side).wait_recv()
+
+            @pl.when(i == 0)
+            def _():
+                pass_y(4)
+                pass_x(1, 2)
+
+            @pl.when(i == 1)
+            def _():
+                pass_y(5)
+                pass_x(3)
+                pass_y(6)
+                pass_x(4)
+
+            @pl.when((n >= 0) & (k == 0))
+            def _():
+                pass_y(j + 7)
+
+                @pl.when(c == 0)
+                def _():
+                    pass_x(5)
+
+            @pl.when((n >= 0) & (k == 1))
+            def _():
+                pass_x(j + 7)
+                arrived(1)
+
+            @pl.when((n >= 0) & (k == 2))
+            def _():
+                pass_x(j + 8)
+
+            @pl.when((n >= 0) & (k == 3))
+            def _():
+                pass_x(j + 9)
+                arrived(3)
+
+            @pl.when((n >= 0) & (k > 0))
             def _():
                 other_load().start()
 
             mine(i)
+
+            @pl.when((n >= 0) & (k == 0))
+            def _():
+                pass_y(j + 8)
+                other_load().start()
+                pass_x(j + 6)
+
+            @pl.when((n >= 0) & (k > 0))
+            def _():
+                pass_y(j + 8 + k)
 
             @pl.when(n >= 0)
             def _():
@@ -667,18 +664,24 @@
                 lax.fori_loop(0, 2, part, 0)
                 store(n).start()
 
+            @pl.when((n >= 0) & (k == 3))
+            def _():
+                pass_x(j + 10)
+
+                @pl.when(n < main - 1)
+                def _():
+                    for p in range(4):
+                        pass_y(j + 12 + p)
+                        pass_x(j + 11 + p)
+
             return carry
 
         lax.fori_loop(0, main + 2, step, 0)
-        last_y(4)
 
         def rest_mine(n, carry):
             mine(n)
-
-            @pl.when(n == main + 2)
-            def _():
-                last_y(5)
-
+            pass_y(last + 3 + n - (main + 2))
+            pass_x(last + 2 + n - (main + 2))
             return carry
 
         lax.fori_loop(main + 2, total, rest_mine, 0)
@@ -686,43 +689,47 @@
             store(main - SP + k).wait()
 
         def piece_load(k, p):
-            at = rows((2 * k + p % 2) * last_rows, last_rows)
-            return load(2 * k + p % 2, wd_rem.at[k, rows(p * last_rows, last_rows), cols(quarter - DOWN_COLS, DOWN_COLS)], w_other.at[at])
+            at = rows((2 * k + p % 2) * part_rows, part_rows)
+            return load(2 * k + p % 2, wd_rem.at[k, rows(p * part_rows, part_rows), cols(quarter - DOWN_COLS, DOWN_COLS)], w_other.at[at])
 
         def piece_dot(k, p):
             piece_load(k, p).wait()
-            at = rows((2 * k + p % 2) * last_rows, last_rows)
-            acc_buf[k] = acc_buf[k] + dot(u_buf[:, cols(half_feat + p * last_rows, last_rows)], w_other[at])
+            at = rows((2 * k + p % 2) * part_rows, part_rows)
+            acc_buf[k] = acc_buf[k] + dot(u_buf[:, cols(half_feat + p * part_rows, part_rows)], w_other[at])
 
         def finish(k):
             o_buf[k] = acc_buf[k].astype(BF16)
             store(main + k).start()
 
         def first_two(p):
-            wl_copy(p, 1).wait_recv()
+            wd_copy(last + p, 1).wait_recv()
             for k in (0, 1):
                 piece_load(k, p).start()
 
         first_two(0)
 
         def last_step(p, carry):
-            @pl.when(p + 6 < LAST_PARTS)
-            def _():
-                last_y(p + 6)
+            for at, m in ((2, 5), (4, 6), (5, 7), (6, 8)):
+
+                @pl.when(p == at)
+                def _():
+                    pass_y(last + m)
 
             piece_dot(0, p)
             piece_dot(1, p)
 
-            @pl.when(p == LAST_PARTS - 1)
+            @pl.when(p == DOWN_PARTS - 1)
             def _():
                 finish(0)
                 finish(1)
 
-            wl_copy(p, 2).wait_recv()
-            wl_copy(p, 3).start()
+            @pl.when(p >= 4)
+            def _():
+                pass_x(last + p)
+
             piece_load(2, p).start()
 
-            @pl.when(p + 1 < LAST_PARTS)
+            @pl.when(p + 1 < DOWN_PARTS)
             def _():
                 first_two(p + 1)
 
@@ -732,16 +739,16 @@
 
             piece_dot(2, p)
 
-            @pl.when(p == LAST_PARTS - 1)
+            @pl.when(p == DOWN_PARTS - 1)
             def _():
                 finish(2)
 
-            wl_copy(p, 3).wait_recv()
+            wd_copy(last + p, 3).wait_recv()
             piece_load(3, p).start()
             return carry
 
-        lax.fori_loop(0, LAST_PARTS, last_step, 0)
-        piece_dot(3, LAST_PARTS - 1)
+        lax.fori_loop(0, DOWN_PARTS, last_step, 0)
+        piece_dot(3, DOWN_PARTS - 1)
         finish(3)
         for k in range(SP):
             store(main + k).wait()
@@ -792,14 +799,20 @@
             wd_copy(m, k).wait_send()
         return carry
 
-    lax.fori_loop(0, DOWN_PARTS * (down_chunks - 1), wd_sent, 0)
-
-    def wl_sent(p, carry):
-        for k in range(SP):
-            wl_copy(p, k).wait_send()
-        return carry
-
-    lax.fori_loop(0, LAST_PARTS, wl_sent, 0)
+    lax.fori_loop(0, DOWN_PARTS * down_chunks, wd_sent, 0)
+
+
+def hand_over(src, dst, buf, in_sem, out_sem):
+    n = src.shape[0]
+    reads = [pltpu.make_async_copy(src.at[r], buf.at[r], in_sem.at[r]) for r in range(n)]
+    writes = [pltpu.make_async_copy(buf.at[r], dst.at[r], out_sem.at[r]) for r in range(n)]
+    for d in reads:
+        d.start()
+    for r in range(n):
+        reads[r].wait()
+        writes[r].start()
+    for d in writes:
+        d.wait()
 
 
 def tables(shard_len):
@@ -843,7 +856,7 @@
         buf(SP * tokens, feat),
     ]
     chunks = FULL_CHUNKS + 2
-    copies = 2 + 6 + 4 + 2 * chunks + 4 * DOWN_PARTS * (quarter // DOWN_COLS - 1) + 4 * LAST_PARTS + 17 * ROW_CHUNKS + 3 * chunks
+    copies = 2 + 6 + 4 + 2 * chunks + 4 * DOWN_PARTS * (quarter // DOWN_COLS) + 17 * ROW_CHUNKS + 3 * chunks
     outs = pl.pallas_call(
         layer_kernel,
         out_shape=shapes,
@@ -860,7 +873,19 @@
         compiler_params=pltpu.CompilerParams(collective_id=0, has_side_effects=True, vmem_limit_bytes=67043328),
         name="decoder_layer",
     )(x_loc.reshape(tokens, dim), norm_attn, norm_mlp, w_query, w_key, w_value, w_out, w_gate, w_up, w_down, jnp.asarray(cos), jnp.asarray(sin))
-    return outs[0].reshape(x_loc.shape)
+    return pl.pallas_call(
+        hand_over,
+        out_shape=buf(*x_loc.shape),
+        in_specs=[ANY],
+        out_specs=ANY,
+        scratch_shapes=[
+            pltpu.VMEM(x_loc.shape, BF16),
+            pltpu.SemaphoreType.DMA((num_rows,)),
+            pltpu.SemaphoreType.DMA((num_rows,)),
+        ],
+        compiler_params=pltpu.CompilerParams(vmem_limit_bytes=67043328),
+        name="hand_over",
+    )(outs[0].reshape(x_loc.shape))
 
 
 def solution(mesh):

time: 1760 us -> 1760 us (level)
  no operation moved by 1% of the time
where the time goes in v4:
time: 1760 us
  Pallas kernels  1760 us (100%)
    pallas_call x1, Pallas kernels, local_layer(): pl.pallas_call(layer_kernel, out_shape=shapes, in_specs=[ANY] * 12, out_s...  1750 us

profile of v4, /device:TPU:0, one launch (start us, length us, event | category | flops | bytes accessed | tf_op | source)
XLA Modules:
  0.0 1760.4 jit_solution(9316130480805608665)
XLA Ops:
  0.0 1751.3 %decoder_layer.1 = (bf16[1152,5120]{1,0:T(8,128)(2,1)}, bf16[2560]{0:T(1024)(128)(2,1)}, bf16[2560]{0:T(1024)(128)(2,1)}, bf16[1152,5120]{1,0:T(8,128)(2,1)}, bf...) custom-call(bf16[1152,5120]{1,0:T(8,128)(2,1)} %bitcast.3, ...), custom_call_target="tpu_custom_call" | custom-call | tf_op jit(solution)/shard_map/decoder_layer/pallas_call | solution.py:860
  1751.3 8.9 hand_over.1

commit v5 on v4

--- a/solution.py
+++ b/solution.py
@@ -48,9 +48,9 @@
     down_chunks = quarter // DOWN_COLS
     part_rows = half_feat // DOWN_PARTS
     heads = eighth // HEAD_DIM
-    rest = feat - FULL_CHUNKS * GATE_COLS
-    sizes = [GATE_COLS] * FULL_CHUNKS + [rest - 128, 128]
-    starts = [GATE_COLS * c for c in range(FULL_CHUNKS)] + [feat - rest, feat - 128]
+    short = (feat - FULL_CHUNKS * GATE_COLS) // 128
+    sizes = [GATE_COLS] * FULL_CHUNKS + [128] * short
+    starts = [sum(sizes[:c]) for c in range(len(sizes))]
     chunks = len(sizes)
 
     y = lax.axis_index("fsdp")
@@ -142,6 +142,17 @@
         here = (pl.ds(k * tokens, tokens), cols(start, size))
         return copy(s_u + 3 * c + k - 1, u_own.at[here], u_got.at[here], to[k])
 
+    def pass_y(*ms):
+        for m in ms:
+            wd_copy(m, 0).wait_recv()
+            wd_copy(m, 2).start()
+            wd_copy(m, 1).start()
+
+    def pass_x(*ms):
+        for m in ms:
+            wd_copy(m, 2).wait_recv()
+            wd_copy(m, 3).start()
+
     for r in range(ROW_CHUNKS):
         x_copy(r).start()
     for d in gain_copies:
@@ -151,9 +162,12 @@
             qkv_copy(j, h).start()
     wo_copy(0).start()
     for c in range(chunks):
+        if c == FULL_CHUNKS:
+            for m in range(DOWN_PARTS):
+                wd_copy(m, 0).start()
         for t in range(2):
             gu_copy(c, t, starts[c], sizes[c]).start()
-    for m in range(DOWN_PARTS * down_chunks):
+    for m in range(DOWN_PARTS, DOWN_PARTS * down_chunks):
         wd_copy(m, 0).start()
     tabs = [load(0, cos, cos_buf), load(1, sin, sin_buf), load(2, gain_attn, gain_a), load(3, gain_mlp, gain_m)]
     for d in tabs:
@@ -466,7 +480,8 @@
                 u_copy(c, 2, start, size).start()
                 u_copy(c, 3, start, size).start()
 
-        def chunk(c, slot, start, size, prefetch):
+        def chunk(c, slot, start, size, prefetch, before, middle, after):
+            before()
             mine, other = w_load(slot, start, size)
             for t in range(2):
                 gu_copy(c, t, start, size).wait_recv()
@@ -490,10 +505,20 @@
                             to[1],
                         ).wait_recv()
 
+                @pl.when(side == 0)
+                def _():
+                    middle()
+
                 run(c, side, slot, start, size)
                 return carry
 
             lax.fori_loop(0, 2, sides, 0)
+            after()
+
+        def at(c, n, work):
+            @pl.when(c == n)
+            def _():
+                work()
 
         for d in w_load(0, 0, GATE_COLS)[0]:
             d.start()
@@ -507,21 +532,47 @@
 
                 @pl.when(c + 1 == FULL_CHUNKS)
                 def _():
-                    for d in w_load((c + 1) % 2, starts[FULL_CHUNKS], sizes[FULL_CHUNKS])[0]:
+                    for d in w_load((c + 1) % 2, starts[FULL_CHUNKS], 128)[0]:
                         d.start()
 
-            chunk(c, c % 2, c * GATE_COLS, GATE_COLS, prefetch)
+            def before():
+                at(c, FULL_CHUNKS - 1, lambda: pass_y(0, 1))
+
+            def middle():
+                at(c, FULL_CHUNKS - 1, lambda: (pass_y(2, 3, 4), pass_x(0)))
+
+            def after():
+                at(c, FULL_CHUNKS - 1, lambda: (pass_y(5, 6, 7), pass_x(1)))
+
+            chunk(c, c % 2, c * GATE_COLS, GATE_COLS, prefetch, before, middle, after)
             return carry
 
         lax.fori_loop(0, FULL_CHUNKS, full, 0)
-        for c in range(FULL_CHUNKS, chunks):
-
-            def prefetch(c=c):
-                if c + 1 < chunks:
-                    for d in w_load((c + 1) % 2, starts[c + 1], sizes[c + 1])[0]:
+
+        def brief(c, carry):
+            def start_of(i):
+                return starts[FULL_CHUNKS] + (i - FULL_CHUNKS) * 128
+
+            def prefetch():
+                @pl.when(c + 1 < chunks)
+                def _():
+                    for d in w_load((c + 1) % 2, start_of(c + 1), 128)[0]:
                         d.start()
 
-            chunk(c, c % 2, starts[c], sizes[c], prefetch)
+            def before():
+                at(c, FULL_CHUNKS, lambda: pass_y(8))
+                at(c, FULL_CHUNKS + 1, lambda: pass_x(4))
+                at(c, FULL_CHUNKS + 2, lambda: pass_x(6))
+
+            def middle():
+                at(c, FULL_CHUNKS, lambda: pass_x(2, 3))
+                at(c, FULL_CHUNKS + 1, lambda: pass_x(5))
+                at(c, FULL_CHUNKS + 2, lambda: (pass_y(9), pass_x(7)))
+
+            chunk(c, c % 2, start_of(c), 128, prefetch, before, middle, lambda: None)
+            return carry
+
+        lax.fori_loop(FULL_CHUNKS, chunks, brief, 0)
 
     def down_phase(u_buf, w_mine, w_other, h_buf, acc_buf, o_buf):
         total = SP * down_chunks
@@ -530,17 +581,6 @@
         last = pieces - DOWN_PARTS
         band = tokens // 2
 
-        def pass_y(*ms):
-            for m in ms:
-                wd_copy(m, 0).wait_recv()
-                wd_copy(m, 2).start()
-                wd_copy(m, 1).start()
-
-        def pass_x(*ms):
-            for m in ms:
-                wd_copy(m, 2).wait_recv()
-                wd_copy(m, 3).start()
-
         def u_load(k):
             sp = sp_of(k)
             at = ((sp // 2 + y) % 2) * half_feat + (sp % 2) * feat
@@ -555,7 +595,7 @@
             return [load(4 + 2 * slot, wd.at[:, here], w_mine.at[slot]), load(5 + 2 * slot, hid.at[0:tokens, here], h_buf.at[slot])]
 
         def store(n):
-            return load(8 + n % SP, o_buf.at[n % SP], out.at[:, out_cols(n)])
+            return load(8 + n % 2, o_buf.at[n % 2], out.at[:, out_cols(n)])
 
         def mine(n):
             @pl.when(n + 1 < total)
@@ -576,117 +616,88 @@
         for d in fetch(0):
             d.start()
         u_load(0).start()
-        pass_y(0, 1, 2)
+        pass_y(10, 11)
+        pass_x(8)
         for k in (1, 2, 3):
             for c in range(chunks):
                 u_copy(c, k, starts[c], sizes[c]).wait_recv()
             u_load(k).start()
-        pass_y(3)
-        pass_x(0)
         for k in range(SP):
             u_load(k).wait()
 
-        def step(i, carry):
-            n = i - 2
+        def other(n):
             c, k = n // SP, n % SP
-            j = DOWN_PARTS * c
-
-            def other_load():
-                return load(12, wd_rem.at[k, :, cols(c * DOWN_COLS, DOWN_COLS)], w_other)
-
-            def arrived(side):
-                for p in range(DOWN_PARTS):
-                    wd_copy(j + p, side).wait_recv()
-
-            @pl.when(i == 0)
-            def _():
-                pass_y(4)
-                pass_x(1, 2)
-
-            @pl.when(i == 1)
-            def _():
-                pass_y(5)
-                pass_x(3)
-                pass_y(6)
-                pass_x(4)
-
-            @pl.when((n >= 0) & (k == 0))
-            def _():
-                pass_y(j + 7)
-
-                @pl.when(c == 0)
+            ready = load(12, wd_rem.at[k, :, cols(c * DOWN_COLS, DOWN_COLS)], w_other)
+            for side in (1, 3):
+
+                @pl.when(k == side)
                 def _():
-                    pass_x(5)
-
-            @pl.when((n >= 0) & (k == 1))
-            def _():
-                pass_x(j + 7)
-                arrived(1)
-
-            @pl.when((n >= 0) & (k == 2))
-            def _():
-                pass_x(j + 8)
-
-            @pl.when((n >= 0) & (k == 3))
-            def _():
-                pass_x(j + 9)
-                arrived(3)
-
-            @pl.when((n >= 0) & (k > 0))
-            def _():
-                other_load().start()
-
-            mine(i)
-
-            @pl.when((n >= 0) & (k == 0))
-            def _():
-                pass_y(j + 8)
-                other_load().start()
-                pass_x(j + 6)
-
-            @pl.when((n >= 0) & (k > 0))
-            def _():
-                pass_y(j + 8 + k)
-
-            @pl.when(n >= 0)
-            def _():
-                other_load().wait()
-
-                @pl.when(n >= SP)
-                def _():
-                    store(n - SP).wait()
-
-                def part(t, c2):
-                    m = rows(t * band, band)
-                    o_buf[n % SP, m] = (acc_buf[n % SP, m] + dot(u_buf[m, half_feat:], w_other[...])).astype(BF16)
+                    for p in range(DOWN_PARTS):
+                        wd_copy(DOWN_PARTS * c + p, side).wait_recv()
+
+            ready.start()
+
+            @pl.when(n >= 2)
+            def _():
+                store(n - 2).wait()
+
+            ready.wait()
+
+            def part(t, carry):
+                m = rows(t * band, band)
+                o_buf[k % 2, m] = (acc_buf[k, m] + dot(u_buf[m, half_feat:], w_other[...])).astype(BF16)
+                return carry
+
+            lax.fori_loop(0, 2, part, 0)
+            store(n).start()
+
+        def first(n, carry):
+            @pl.when(n < 5)
+            def _():
+                pass_y(12 + n)
+                pass_x(9 + n)
+
+            @pl.when(n == 6)
+            def _():
+                pass_y(17)
+                pass_x(14)
+
+            mine(n)
+
+            @pl.when(n < SP)
+            def _():
+                other(n)
+
+            return carry
+
+        def slot(m, carry):
+            c, r = (m - 8) // 9, (m - 8) % 9
+            pass_y(m + 1)
+            pass_x(m - 2)
+            two = 2 * (r // 3)
+
+            @pl.when((r == 0) | (r == 3))
+            def _():
+                def run(k, c2):
+                    other(SP * c + two + k)
                     return c2
 
-                lax.fori_loop(0, 2, part, 0)
-                store(n).start()
-
-            @pl.when((n >= 0) & (k == 3))
-            def _():
-                pass_x(j + 10)
-
-                @pl.when(n < main - 1)
-                def _():
-                    for p in range(4):
-                        pass_y(j + 12 + p)
-                        pass_x(j + 11 + p)
+                lax.fori_loop(0, 2, run, 0)
+
+            @pl.when((r == 1) | (r == 4))
+            def _():
+                def run(k, c2):
+                    mine(SP * (c + 1) + two + k)
+                    return c2
+
+                lax.fori_loop(0, 2, run, 0)
 
             return carry
 
-        lax.fori_loop(0, main + 2, step, 0)
-
-        def rest_mine(n, carry):
-            mine(n)
-            pass_y(last + 3 + n - (main + 2))
-            pass_x(last + 2 + n - (main + 2))
-            return carry
-
-        lax.fori_loop(main + 2, total, rest_mine, 0)
-        for k in range(SP):
-            store(main - SP + k).wait()
+        lax.fori_loop(0, 2 * SP, first, 0)
+        if down_chunks > 2:
+            lax.fori_loop(2 * DOWN_PARTS - 1, last + 4, slot, 0)
+        next_y, next_x = (5, 2) if down_chunks > 2 else (9, 6)
 
         def piece_load(k, p):
             at = rows((2 * k + p % 2) * part_rows, part_rows)
@@ -698,7 +709,8 @@
             acc_buf[k] = acc_buf[k] + dot(u_buf[:, cols(half_feat + p * part_rows, part_rows)], w_other[at])
 
         def finish(k):
-            o_buf[k] = acc_buf[k].astype(BF16)
+            store(main + k - 2).wait()
+            o_buf[k % 2] = acc_buf[k].astype(BF16)
             store(main + k).start()
 
         def first_two(p):
@@ -709,11 +721,9 @@
         first_two(0)
 
         def last_step(p, carry):
-            for at, m in ((2, 5), (4, 6), (5, 7), (6, 8)):
-
-                @pl.when(p == at)
-                def _():
-                    pass_y(last + m)
+            @pl.when(p + next_y < DOWN_PARTS)
+            def _():
+                pass_y(last + next_y + p)
 
             piece_dot(0, p)
             piece_dot(1, p)
@@ -723,7 +733,7 @@
                 finish(0)
                 finish(1)
 
-            @pl.when(p >= 4)
+            @pl.when(p >= next_x)
             def _():
                 pass_x(last + p)
 
@@ -750,7 +760,7 @@
         lax.fori_loop(0, DOWN_PARTS, last_step, 0)
         piece_dot(3, DOWN_PARTS - 1)
         finish(3)
-        for k in range(SP):
+        for k in (2, 3):
             store(main + k).wait()
 
     lax.fori_loop(0, ROW_CHUNKS, own_a, 0)
@@ -765,7 +775,7 @@
         pltpu.VMEM((half_feat, DOWN_COLS), BF16),
         pltpu.VMEM((2, tokens, DOWN_COLS), BF16),
         pltpu.VMEM((SP, tokens, DOWN_COLS), F32),
-        pltpu.VMEM((SP, tokens, DOWN_COLS), BF16),
+        pltpu.VMEM((2, tokens, DOWN_COLS), BF16),
     )
 
     for d in gain_copies:
@@ -855,7 +865,7 @@
         buf(SP * tokens, feat),
         buf(SP * tokens, feat),
     ]
-    chunks = FULL_CHUNKS + 2
+    chunks = FULL_CHUNKS + (feat - FULL_CHUNKS * GATE_COLS) // 128
     copies = 2 + 6 + 4 + 2 * chunks + 4 * DOWN_PARTS * (quarter // DOWN_COLS) + 17 * ROW_CHUNKS + 3 * chunks
     outs = pl.pallas_call(
         layer_kernel,

time: 1760 us -> 1760 us (level)
  no operation moved by 1% of the time
where the time goes in v5:
time: 1760 us
  Pallas kernels  1760 us (100%)
    pallas_call x1, Pallas kernels, local_layer(): pl.pallas_call(layer_kernel, out_shape=shapes, in_specs=[ANY] * 12, out_s...  1750 us

profile of v5, /device:TPU:0, one launch (start us, length us, event | category | flops | bytes accessed | tf_op | source)
XLA Modules:
  0.0 1755.6 jit_solution(16522508320022072202)
XLA Ops:
  0.0 1746.6 %decoder_layer.1 = (bf16[1152,5120]{1,0:T(8,128)(2,1)}, bf16[2560]{0:T(1024)(128)(2,1)}, bf16[2560]{0:T(1024)(128)(2,1)}, bf16[1152,5120]{1,0:T(8,128)(2,1)}, bf...) custom-call(bf16[1152,5120]{1,0:T(8,128)(2,1)} %bitcast.3, ...), custom_call_target="tpu_custom_call" | custom-call | tf_op jit(solution)/shard_map/decoder_layer/pallas_call | solution.py:870
  1746.6 8.9 hand_over.1

commit v6 on v5

--- a/solution.py
+++ b/solution.py
@@ -26,6 +26,7 @@
 FULL_CHUNKS = 8
 DOWN_COLS = 256
 DOWN_PARTS = 9
+LAST_CUTS = 3
 ROW_CHUNKS = 3
 
 
@@ -76,7 +77,7 @@
         return used[0] - n
 
     s_gain, s_qkv, s_wo, s_gu = slots(2), slots(6), slots(4), slots(2 * chunks)
-    s_wd = slots(4 * DOWN_PARTS * down_chunks)
+    s_wd, s_wl = slots(4 * DOWN_PARTS * down_chunks), slots(4 * LAST_CUTS)
     s_x, s_a, s_b = slots(ROW_CHUNKS), slots(2 * ROW_CHUNKS), slots(2 * ROW_CHUNKS)
     s_o, s_u = slots(12 * ROW_CHUNKS), slots(3 * chunks)
 
@@ -119,6 +120,23 @@
             return copy(s_wd + 4 * m, wd.at[part, cols(me * quarter + col, DOWN_COLS)], wd_rem.at[0, part, cols(col, DOWN_COLS)], to_y)
         here = (part, cols(col, DOWN_COLS))
         return copy(s_wd + 4 * m + k, wd_rem.at[(2 if k == 3 else 0, *here)], wd_rem.at[(k, *here)], to[2] if k == 2 else to[1])
+
+    end = DOWN_PARTS * down_chunks - 1
+
+    def last_copy(i, k):
+        n = part_rows // LAST_CUTS
+        part, col = rows((DOWN_PARTS - 1) * part_rows + i * n, n), quarter - DOWN_COLS
+        if k == 0:
+            return copy(s_wl + 4 * i, wd.at[part, cols(me * quarter + col, DOWN_COLS)], wd_rem.at[0, part, cols(col, DOWN_COLS)], to_y)
+        here = (part, cols(col, DOWN_COLS))
+        return copy(s_wl + 4 * i + k, wd_rem.at[(2 if k == 3 else 0, *here)], wd_rem.at[(k, *here)], to[2] if k == 2 else to[1])
+
+    def wd_arrived(m, k):
+        if isinstance(m, int) and m == end:
+            for i in range(LAST_CUTS):
+                last_copy(i, k).wait_recv()
+        else:
+            wd_copy(m, k).wait_recv()
 
     def act_copy(base, ref, piece, r):
         return copy(
@@ -142,16 +160,23 @@
         here = (pl.ds(k * tokens, tokens), cols(start, size))
         return copy(s_u + 3 * c + k - 1, u_own.at[here], u_got.at[here], to[k])
 
+    def cuts(m):
+        if isinstance(m, int) and m == end:
+            return [functools.partial(last_copy, i) for i in range(LAST_CUTS)]
+        return [functools.partial(wd_copy, m)]
+
     def pass_y(*ms):
         for m in ms:
-            wd_copy(m, 0).wait_recv()
-            wd_copy(m, 2).start()
-            wd_copy(m, 1).start()
+            for piece in cuts(m):
+                piece(0).wait_recv()
+                piece(2).start()
+                piece(1).start()
 
     def pass_x(*ms):
         for m in ms:
-            wd_copy(m, 2).wait_recv()
-            wd_copy(m, 3).start()
+            for piece in cuts(m):
+                piece(2).wait_recv()
+                piece(3).start()
 
     for r in range(ROW_CHUNKS):
         x_copy(r).start()
@@ -167,8 +192,10 @@
                 wd_copy(m, 0).start()
         for t in range(2):
             gu_copy(c, t, starts[c], sizes[c]).start()
-    for m in range(DOWN_PARTS, DOWN_PARTS * down_chunks):
+    for m in range(DOWN_PARTS, end):
         wd_copy(m, 0).start()
+    for i in range(LAST_CUTS):
+        last_copy(i, 0).start()
     tabs = [load(0, cos, cos_buf), load(1, sin, sin_buf), load(2, gain_attn, gain_a), load(3, gain_mlp, gain_m)]
     for d in tabs:
         d.start()
@@ -577,8 +604,7 @@
     def down_phase(u_buf, w_mine, w_other, h_buf, acc_buf, o_buf):
         total = SP * down_chunks
         main = total - SP
-        pieces = DOWN_PARTS * down_chunks
-        last = pieces - DOWN_PARTS
+        last = end + 1 - DOWN_PARTS
         band = tokens // 2
 
         def u_load(k):
@@ -651,18 +677,22 @@
             lax.fori_loop(0, 2, part, 0)
             store(n).start()
 
+        pieces = DOWN_PARTS * down_chunks
+
+        def passes(n, table):
+            for when, (m_y, m_x) in table.items():
+
+                @pl.when(n == when)
+                def _():
+                    if m_y < pieces:
+                        pass_y(m_y)
+                    if m_x is not None:
+                        pass_x(m_x)
+
         def first(n, carry):
-            @pl.when(n < 5)
-            def _():
-                pass_y(12 + n)
-                pass_x(9 + n)
-
-            @pl.when(n == 6)
-            def _():
-                pass_y(17)
-                pass_x(14)
-
+            passes(n, {0: (12, None), 2: (15, 11), 3: (16, 12), 5: (18, 14), 7: (19, 15)})
             mine(n)
+            passes(n, {0: (13, 9), 1: (14, 10), 3: (17, 13)})
 
             @pl.when(n < SP)
             def _():
@@ -670,10 +700,11 @@
 
             return carry
 
-        def slot(m, carry):
+        def slot(i, carry):
+            m = 17 + i + 2 * ((i + 14) // 21)
             c, r = (m - 8) // 9, (m - 8) % 9
-            pass_y(m + 1)
-            pass_x(m - 2)
+            pass_y(20 + i)
+            pass_x(16 + i)
             two = 2 * (r // 3)
 
             @pl.when((r == 0) | (r == 3))
@@ -696,8 +727,8 @@
 
         lax.fori_loop(0, 2 * SP, first, 0)
         if down_chunks > 2:
-            lax.fori_loop(2 * DOWN_PARTS - 1, last + 4, slot, 0)
-        next_y, next_x = (5, 2) if down_chunks > 2 else (9, 6)
+            lax.fori_loop(0, last + 4 - 19, slot, 0)
+        next_y, next_x = (5, 1) if down_chunks > 2 else (9, 7)
 
         def piece_load(k, p):
             at = rows((2 * k + p % 2) * part_rows, part_rows)
@@ -714,16 +745,31 @@
             store(main + k).start()
 
         def first_two(p):
-            wd_copy(last + p, 1).wait_recv()
+            if isinstance(p, int):
+                wd_arrived(last + p, 1)
+            else:
+
+                @pl.when(p < DOWN_PARTS - 1)
+                def _():
+                    wd_arrived(last + p, 1)
+
+                @pl.when(p == DOWN_PARTS - 1)
+                def _():
+                    wd_arrived(end, 1)
+
             for k in (0, 1):
                 piece_load(k, p).start()
 
         first_two(0)
 
         def last_step(p, carry):
-            @pl.when(p + next_y < DOWN_PARTS)
+            @pl.when(p + next_y < DOWN_PARTS - 1)
             def _():
                 pass_y(last + next_y + p)
+
+            @pl.when(p + next_y == DOWN_PARTS - 1)
+            def _():
+                pass_y(end)
 
             piece_dot(0, p)
             piece_dot(1, p)
@@ -733,10 +779,14 @@
                 finish(0)
                 finish(1)
 
-            @pl.when(p >= next_x)
+            @pl.when((p >= next_x) & (p < DOWN_PARTS - 1))
             def _():
                 pass_x(last + p)
 
+            @pl.when(p == DOWN_PARTS - 1)
+            def _():
+                pass_x(end)
+
             piece_load(2, p).start()
 
             @pl.when(p + 1 < DOWN_PARTS)
@@ -753,7 +803,14 @@
             def _():
                 finish(2)
 
-            wd_copy(last + p, 3).wait_recv()
+            @pl.when(p < DOWN_PARTS - 1)
+            def _():
+                wd_arrived(last + p, 3)
+
+            @pl.when(p == DOWN_PARTS - 1)
+            def _():
+                wd_arrived(end, 3)
+
             piece_load(3, p).start()
             return carry
 
@@ -809,7 +866,10 @@
             wd_copy(m, k).wait_send()
         return carry
 
-    lax.fori_loop(0, DOWN_PARTS * down_chunks, wd_sent, 0)
+    lax.fori_loop(0, end, wd_sent, 0)
+    for i in range(LAST_CUTS):
+        for k in range(SP):
+            last_copy(i, k).wait_send()
 
 
 def hand_over(src, dst, buf, in_sem, out_sem):
@@ -866,7 +926,7 @@
         buf(SP * tokens, feat),
     ]
     chunks = FULL_CHUNKS + (feat - FULL_CHUNKS * GATE_COLS) // 128
-    copies = 2 + 6 + 4 + 2 * chunks + 4 * DOWN_PARTS * (quarter // DOWN_COLS) + 17 * ROW_CHUNKS + 3 * chunks
+    copies = 2 + 6 + 4 + 2 * chunks + 4 * DOWN_PARTS * (quarter // DOWN_COLS) + 4 * LAST_CUTS + 17 * ROW_CHUNKS + 3 * chunks
     outs = pl.pallas_call(
         layer_kernel,
         out_shape=shapes,

time: 1760 us -> 1760 us (level)
  no operation moved by 1% of the time
where the time goes in v6:
time: 1760 us; the launch traced here: 1750 us
  Pallas kernels  1750 us (99%)
    pallas_call x1, Pallas kernels, local_layer(): pl.pallas_call(layer_kernel, out_shape=shapes, in_specs=[ANY] * 12, out_s...  1740 us

profile of v6, /device:TPU:0, one launch (start us, length us, event | category | flops | bytes accessed | tf_op | source)
XLA Modules:
  0.0 1752.8 jit_solution(7668277475220460627)
XLA Ops:
  0.0 1743.7 %decoder_layer.1 = (bf16[1152,5120]{1,0:T(8,128)(2,1)}, bf16[2560]{0:T(1024)(128)(2,1)}, bf16[2560]{0:T(1024)(128)(2,1)}, bf16[1152,5120]{1,0:T(8,128)(2,1)}, bf...) custom-call(bf16[1152,5120]{1,0:T(8,128)(2,1)} %bitcast.3, ...), custom_call_target="tpu_custom_call" | custom-call | tf_op jit(solution)/shard_map/decoder_layer/pallas_call | solution.py:930
  1743.7 8.9 hand_over.1

commit v7 on v6

--- a/solution.py
+++ b/solution.py
@@ -26,7 +26,7 @@
 FULL_CHUNKS = 8
 DOWN_COLS = 256
 DOWN_PARTS = 9
-LAST_CUTS = 3
+LAST_CUTS = 1
 ROW_CHUNKS = 3
 
 
@@ -128,8 +128,10 @@
         part, col = rows((DOWN_PARTS - 1) * part_rows + i * n, n), quarter - DOWN_COLS
         if k == 0:
             return copy(s_wl + 4 * i, wd.at[part, cols(me * quarter + col, DOWN_COLS)], wd_rem.at[0, part, cols(col, DOWN_COLS)], to_y)
+        if k == 2:
+            return copy(s_wl + 4 * i + 2, wd.at[part, cols(sp_of(2) * quarter + col, DOWN_COLS)], wd_rem.at[2, part, cols(col, DOWN_COLS)], to_y)
         here = (part, cols(col, DOWN_COLS))
-        return copy(s_wl + 4 * i + k, wd_rem.at[(2 if k == 3 else 0, *here)], wd_rem.at[(k, *here)], to[2] if k == 2 else to[1])
+        return copy(s_wl + 4 * i + k, wd_rem.at[(k - 1, *here)], wd_rem.at[(k, *here)], to[1])
 
     def wd_arrived(m, k):
         if isinstance(m, int) and m == end:
@@ -169,7 +171,8 @@
         for m in ms:
             for piece in cuts(m):
                 piece(0).wait_recv()
-                piece(2).start()
+                if not (isinstance(m, int) and m == end):
+                    piece(2).start()
                 piece(1).start()
 
     def pass_x(*ms):
@@ -194,8 +197,9 @@
             gu_copy(c, t, starts[c], sizes[c]).start()
     for m in range(DOWN_PARTS, end):
         wd_copy(m, 0).start()
-    for i in range(LAST_CUTS):
-        last_copy(i, 0).start()
+    for k in (0, 2):
+        for i in range(LAST_CUTS):
+            last_copy(i, k).start()
     tabs = [load(0, cos, cos_buf), load(1, sin, sin_buf), load(2, gain_attn, gain_a), load(3, gain_mlp, gain_m)]
     for d in tabs:
         d.start()
@@ -634,7 +638,7 @@
 
             def part(t, carry):
                 m = rows(t * band, band)
-                acc_buf[n % SP, m] = h_buf[n % 2, m].astype(F32) + dot(u_buf[m, 0:half_feat], w_mine[n % 2])
+                acc_buf[n % (2 * SP), m] = h_buf[n % 2, m].astype(F32) + dot(u_buf[m, 0:half_feat], w_mine[n % 2])
                 return carry
 
             lax.fori_loop(0, 2, part, 0)
@@ -671,7 +675,7 @@
 
             def part(t, carry):
                 m = rows(t * band, band)
-                o_buf[k % 2, m] = (acc_buf[k, m] + dot(u_buf[m, half_feat:], w_other[...])).astype(BF16)
+                o_buf[k % 2, m] = (acc_buf[n % (2 * SP), m] + dot(u_buf[m, half_feat:], w_other[...])).astype(BF16)
                 return carry
 
             lax.fori_loop(0, 2, part, 0)
@@ -715,10 +719,10 @@
 
                 lax.fori_loop(0, 2, run, 0)
 
-            @pl.when((r == 1) | (r == 4))
+            @pl.when((((r == 1) | (r == 4)) & (c < 3)) | (((r == 5) | (r == 6)) & (c == 1)))
             def _():
                 def run(k, c2):
-                    mine(SP * (c + 1) + two + k)
+                    mine(2 * SP * c + two + 2 * (r // 5) + k)
                     return c2
 
                 lax.fori_loop(0, 2, run, 0)
@@ -728,7 +732,9 @@
         lax.fori_loop(0, 2 * SP, first, 0)
         if down_chunks > 2:
             lax.fori_loop(0, last + 4 - 19, slot, 0)
-        next_y, next_x = (5, 1) if down_chunks > 2 else (9, 7)
+        next_y, next_x = (4, 1) if down_chunks > 2 else (9, 7)
+
+        base = main % (2 * SP)
 
         def piece_load(k, p):
             at = rows((2 * k + p % 2) * part_rows, part_rows)
@@ -737,11 +743,11 @@
         def piece_dot(k, p):
             piece_load(k, p).wait()
             at = rows((2 * k + p % 2) * part_rows, part_rows)
-            acc_buf[k] = acc_buf[k] + dot(u_buf[:, cols(half_feat + p * part_rows, part_rows)], w_other[at])
+            acc_buf[base + k] = acc_buf[base + k] + dot(u_buf[:, cols(half_feat + p * part_rows, part_rows)], w_other[at])
 
         def finish(k):
             store(main + k - 2).wait()
-            o_buf[k % 2] = acc_buf[k].astype(BF16)
+            o_buf[k % 2] = acc_buf[base + k].astype(BF16)
             store(main + k).start()
 
         def first_two(p):
@@ -763,7 +769,7 @@
         first_two(0)
 
         def last_step(p, carry):
-            @pl.when(p + next_y < DOWN_PARTS - 1)
+            @pl.when((p > 0) & (p + next_y < DOWN_PARTS - 1))
             def _():
                 pass_y(last + next_y + p)
 
@@ -831,7 +837,7 @@
         pltpu.VMEM((2, half_feat, DOWN_COLS), BF16),
         pltpu.VMEM((half_feat, DOWN_COLS), BF16),
         pltpu.VMEM((2, tokens, DOWN_COLS), BF16),
-        pltpu.VMEM((SP, tokens, DOWN_COLS), F32),
+        pltpu.VMEM((2 * SP, tokens, DOWN_COLS), F32),
         pltpu.VMEM((2, tokens, DOWN_COLS), BF16),
     )
 

time: 1760 us -> 1750 us (level)
  no operation moved by 1% of the time
where the time goes in v7:
time: 1750 us
  Pallas kernels  1750 us (100%)
    pallas_call x1, Pallas kernels, local_layer(): pl.pallas_call(layer_kernel, out_shape=shapes, in_specs=[ANY] * 12, out_s...  1740 us

profile of v7, /device:TPU:0, one launch (start us, length us, event | category | flops | bytes accessed | tf_op | source)
XLA Modules:
  0.0 1748.5 jit_solution(13966449350970620862)
XLA Ops:
  0.0 1739.5 %decoder_layer.1 = (bf16[1152,5120]{1,0:T(8,128)(2,1)}, bf16[2560]{0:T(1024)(128)(2,1)}, bf16[2560]{0:T(1024)(128)(2,1)}, bf16[1152,5120]{1,0:T(8,128)(2,1)}, bf...) custom-call(bf16[1152,5120]{1,0:T(8,128)(2,1)} %bitcast.3, ...), custom_call_target="tpu_custom_call" | custom-call | tf_op jit(solution)/shard_map/decoder_layer/pallas_call | solution.py:936
  1739.5 8.9 hand_over.1
